TPU v7x, 32 devices: a whole 2x2x4 slice. The times are simulated.
32 devices in a mesh: dp: 8 (over z, x), patch: 4 (over y, core).
Axes of the slice: x: 2, y: 2, z: 4, core: 2. Of those that a mesh axis runs over, the one named last changes fastest.
Arguments:
- token_ids: int32 [128], replicated, may hold values from 0 to 31999
- parents: int32 [128], replicated, may hold values from 0 to 3
- embedding: bfloat16 [32000, 1024], P('dp'), may hold values from -6 to 6
- self_gain: bfloat16 [1024], replicated, may hold values from 0.25 to 1.75
- query_weight: bfloat16 [1024, 1024], P(None, 'patch'), may hold values from -0.1875 to 0.1875
- key_weight: bfloat16 [1024, 1024], P(None, 'patch'), may hold values from -0.1875 to 0.1875
- value_weight: bfloat16 [1024, 1024], P(None, 'patch'), may hold values from -0.1875 to 0.1875
- output_weight: bfloat16 [1024, 1024], P('patch'), may hold values from -0.75 to 0.75
- past_keys: bfloat16 [128, 128, 1024], P('dp', None, 'patch'), may hold values from -200 to 200
- past_values: bfloat16 [128, 128, 1024], P('dp', None, 'patch'), may hold values from -6 to 6
- cross_gain: bfloat16 [1024], replicated, may hold values from 0.25 to 1.75
- cross_query: bfloat16 [1024, 1024], replicated, may hold values from -0.1875 to 0.1875
- cross_output: bfloat16 [1024, 1024], replicated, may hold values from -0.75 to 0.75
- image_keys: bfloat16 [8, 16, 256, 1024], P('dp', None, 'patch'), may hold values from -260 to 260
- image_values: bfloat16 [8, 16, 256, 1024], P('dp', None, 'patch'), may hold values from -6 to 6
Outputs:
- hidden: bfloat16 [128, 1024], P('dp')
- new_keys: bfloat16 [128, 1024], P('dp', 'patch')
- new_values: bfloat16 [128, 1024], P('dp', 'patch')
Inputs may be any that keep to these rules, and one draw needn't show every extreme that they name: `parents`: a beam of the row's own image.
All inputs are finite; a program needn't handle non-finite values.
Results may differ from a plain program's by a relative error of at most 0.019.
The roundings to bfloat16 on the way count: a program that leaves them out, or rounds other values in their place, can miss the bound.
Values may be sent and summed in bfloat16 or wider, within the bound.
No kernel may reach another device: no remote copies, remote signals or barrier semaphores. Data moves between devices by JAX's collectives and lax.ppermute only.
A program may use at most 64 MiB of HBM per device.

v0:
```python
import math

import jax
import jax.numpy as jnp
from jax import lax
from jax.sharding import PartitionSpec as P

D = 1024
HEADS = 16
BEAMS = 4


def from_partner(value, axis, distance):
    mask = 2**distance
    pairs = [(source, source ^ mask) for source in range(lax.axis_size(axis))]
    return lax.ppermute(value, axis, pairs)


def joined(x, axis, combine):
    everything = jax.tree.map(lambda part: lax.all_gather(part, axis), x)
    first = jax.tree.map(lambda part: part[0], everything)

    def step(k, so_far):
        return combine(so_far, jax.tree.map(lambda part: part[k], everything))

    return lax.fori_loop(1, lax.axis_size(axis), step, first)


def normalize(inputs, gains):
    factor = lax.rsqrt(jnp.mean(inputs * inputs, axis=-1, keepdims=True) + 1e-06)
    return (inputs * factor * gains.astype(jnp.float32)).astype(jnp.bfloat16)


def combine(former, latter):
    peak_former, total_former, sum_former = former
    peak_latter, total_latter, sum_latter = latter
    peaks = jnp.maximum(peak_former, peak_latter)
    former_scale = jnp.exp(peak_former - peaks)
    latter_scale = jnp.exp(peak_latter - peaks)
    heads_count = peaks.shape[-1]
    count_rows = peaks.shape[0]
    sums = (
        sum_former.reshape(count_rows, heads_count, -1) * former_scale[..., None]
        + sum_latter.reshape(count_rows, heads_count, -1) * latter_scale[..., None]
    )
    return (
        peaks,
        total_former * former_scale + total_latter * latter_scale,
        sums.reshape(count_rows, -1),
    )


def beam_collect(pieces, concat_dim):
    for bit_index in range(2):
        partner = from_partner(pieces, "dp", bit_index)
        upper_bit = lax.axis_index("dp") // 2**bit_index % 2
        pieces = jnp.where(
            upper_bit == 1,
            jnp.concatenate([partner, pieces], concat_dim),
            jnp.concatenate([pieces, partner], concat_dim),
        )
    return pieces


def beam_reduce(partial_value):
    for bit_index in (1, 0):
        upper_bit = lax.axis_index("dp") // 2**bit_index % 2
        half_rows = partial_value[0].shape[0] // 2
        keep_part = tuple(
            (
                lax.dynamic_slice_in_dim(member, upper_bit * half_rows, half_rows, 0)
                for member in partial_value
            )
        )
        send_part = tuple(
            (
                lax.dynamic_slice_in_dim(member, (1 - upper_bit) * half_rows, half_rows, 0)
                for member in partial_value
            )
        )
        received = from_partner(send_part, "dp", bit_index)
        partial_value = combine(keep_part, received)
    return partial_value


def patch_merge(partial_value):
    return joined(partial_value, "patch", combine)


def shards(
    token_ids,
    parents,
    embedding,
    self_gain,
    query_weight,
    key_weight,
    value_weight,
    output_weight,
    past_keys,
    past_values,
    cross_gain,
    cross_query,
    cross_output,
    image_keys,
    image_values,
):
    row_count = past_keys.shape[0]
    length = past_keys.shape[1]
    width_here = query_weight.shape[1]
    head_size = D // HEADS
    heads_here = width_here // head_size
    scaling = 1.0 / math.sqrt(head_size)
    position = lax.axis_index("dp")
    slab = embedding.shape[0]
    vocab_ids = position * slab + jnp.arange(slab, dtype=jnp.int32)
    onehot_table = (token_ids[:, None] == vocab_ids[None, :]).astype(jnp.bfloat16)
    tokens = lax.psum_scatter(
        jnp.dot(onehot_table, embedding, preferred_element_type=jnp.float32),
        "dp",
        scatter_dimension=0,
        tiled=True,
    )
    normed = normalize(tokens, self_gain)
    queries = jnp.dot(normed, query_weight, preferred_element_type=jnp.float32).astype(jnp.bfloat16)
    new_key = jnp.dot(normed, key_weight, preferred_element_type=jnp.float32).astype(jnp.bfloat16)
    new_value = jnp.dot(normed, value_weight, preferred_element_type=jnp.float32).astype(
        jnp.bfloat16
    )
    query_heads = queries.reshape(row_count, heads_here, head_size)
    key_heads = new_key.reshape(row_count, heads_here, head_size)
    value_heads = new_value.reshape(row_count, heads_here, head_size)
    own_score = (
        jnp.sum(query_heads.astype(jnp.float32) * key_heads.astype(jnp.float32), axis=-1) * scaling
    )
    paired = jnp.stack([queries, new_key], 0)
    gathered = beam_collect(paired, 1).reshape(2, BEAMS, row_count, heads_here, head_size)
    gathered_queries = gathered[0]
    gathered_keys = gathered[1]
    own_every = (
        jnp.sum(gathered_queries.astype(jnp.float32) * gathered_keys.astype(jnp.float32), axis=-1)
        * scaling
    )
    block_start = position // BEAMS * BEAMS * row_count
    block_parents = lax.dynamic_slice_in_dim(parents, block_start, BEAMS * row_count, 0).reshape(
        BEAMS, row_count
    )
    living = (block_parents == position % BEAMS).astype(jnp.float32)
    old_keys = past_keys.reshape(row_count, length, heads_here, head_size)
    old_values = past_values.reshape(row_count, length, heads_here, head_size)
    scores = (
        jnp.einsum(
            "bihe,ilhe->bihl", gathered_queries, old_keys, preferred_element_type=jnp.float32
        )
        * scaling
    )
    maxima = jnp.maximum(jnp.max(scores, axis=-1), own_every)
    powers = jnp.exp(scores - maxima[..., None]) * living[:, :, None, None]
    totals = jnp.sum(powers, axis=-1) + jnp.exp(own_every - maxima) * living[:, :, None]
    numerators = jnp.einsum(
        "bihl,ilhe->bihe",
        powers.astype(jnp.bfloat16),
        old_values,
        preferred_element_type=jnp.float32,
    )
    partial_value = (
        jnp.where(living[:, :, None] > 0.5, maxima, -1e30).reshape(BEAMS * row_count, heads_here),
        totals.reshape(BEAMS * row_count, heads_here),
        numerators.reshape(BEAMS * row_count, width_here),
    )
    peaks, sums, weighted = beam_reduce(partial_value)
    own_weight = jnp.exp(own_score - peaks).astype(jnp.bfloat16).astype(jnp.float32)
    weighted = weighted.reshape(row_count, heads_here, head_size) + own_weight[
        ..., None
    ] * value_heads.astype(jnp.float32)
    self_context = weighted / sums[..., None]
    self_context = self_context.reshape(row_count, width_here).astype(jnp.bfloat16)
    middle = tokens + lax.psum(
        jnp.dot(self_context, output_weight, preferred_element_type=jnp.float32), "patch"
    )
    probes = jnp.dot(
        normalize(middle, cross_gain), cross_query, preferred_element_type=jnp.float32
    ).astype(jnp.bfloat16)
    every_probe = beam_collect(probes, 0).reshape(BEAMS, row_count, HEADS, head_size)
    patch_count = image_keys.shape[2]
    patch_keys = image_keys.reshape(row_count, patch_count, HEADS, head_size)
    patch_values = image_values.reshape(row_count, patch_count, HEADS, head_size)
    cross_scores = (
        jnp.einsum("bihe,iphe->bihp", every_probe, patch_keys, preferred_element_type=jnp.float32)
        * scaling
    )
    cross_peaks = jnp.max(cross_scores, axis=-1)
    cross_powers = jnp.exp(cross_scores - cross_peaks[..., None])
    cross_totals = jnp.sum(cross_powers, axis=-1)
    cross_sums = jnp.einsum(
        "bihp,iphe->bihe",
        cross_powers.astype(jnp.bfloat16),
        patch_values,
        preferred_element_type=jnp.float32,
    )
    partial_value = (
        cross_peaks.reshape(BEAMS * row_count, HEADS),
        cross_totals.reshape(BEAMS * row_count, HEADS),
        cross_sums.reshape(BEAMS * row_count, D),
    )
    partial_value = beam_reduce(patch_merge(partial_value))
    cross_context = (
        (partial_value[2].reshape(row_count, HEADS, head_size) / partial_value[1][..., None])
        .reshape(row_count, D)
        .astype(jnp.bfloat16)
    )
    hidden = (
        middle + jnp.dot(cross_context, cross_output, preferred_element_type=jnp.float32)
    ).astype(jnp.bfloat16)
    return (hidden, new_key, new_value)


def solution(mesh):
    in_specs = (
        P(),
        P(),
        P("dp", None),
        P(),
        P(None, "patch"),
        P(None, "patch"),
        P(None, "patch"),
        P("patch", None),
        P("dp", None, "patch"),
        P("dp", None, "patch"),
        P(),
        P(),
        P(),
        P("dp", None, "patch", None),
        P("dp", None, "patch", None),
    )
    out_specs = (P("dp", None), P("dp", "patch"), P("dp", "patch"))
    return jax.shard_map(shards, mesh=mesh, in_specs=in_specs, out_specs=out_specs, check_vma=False)
```

profile of v0, /device:TPU:0, one launch (start us, length us, event | category | flops | bytes accessed | tf_op | source)
XLA Modules:
  0.0 208.8 jit_solution(12373102557429961516)
XLA Ops:
  7.3 5.6 %fusion.7 = f32[128,1024]{1,0:T(8,128)} fusion(bf16[4000,1024]{1,0:T(8,128)(2,1)} %param.19, s32[4000]{0:T(1024)S(1)} %iota_add_fusion, s32[128]{0:T(128)} %param.17), kind=kOutput, calls=%fused_computation.12 | convolution fusion | flops 1049088000 | bytes 8732800 | tf_op jit(solution)/shard_map/dot_general | solution.py:118
  13.0 65.4 %reduce-scatter.2.cloned.1.call-done = f32[16,1024]{1,0:T(8,128)} async-done(((f32[128,1024]{1,0:T(8,128)}), f32[16,1024]{1,0:T(8,128)}) %reduce-scatter.2.cloned.1.call-update) | async-done | bytes 65552 | tf_op jit(solution)/shard_map/reduce_scatter | solution.py:117
  78.4 1.0 multiply_reduce_fusion.2
  79.4 0.9 multiply_convert_fusion.1
  80.7 1.4 collective-permute-start
  82.1 1.6 copy.108
  83.9 2.3 %copy.114 = bf16[16,128,256]{1,2,0:T(8,128)(2,1)} copy(bf16[16,128,256]{2,1,0:T(8,128)(2,1)} %param.26) | data formatting | bytes 2097152 | tf_op args[9]
  86.2 1.6 collective-permute-start.1
  87.8 1.2 convolution_convert_fusion.1
  89.2 0.9 collective-permute-done.1
  91.9 1.9 convolution_bitcast_fusion
  94.5 1.6 collective-permute-start.2
  96.5 1.5 collective-permute-start.3
  98.3 1.6 collective-permute-done.6
  100.2 0.6 collective-permute-start.4
  100.8 1.5 collective-permute-start.7
  102.4 0.6 collective-permute-start.5
  102.9 1.0 collective-permute-done.4
  105.2 1.0 collective-permute-done.5
  106.2 0.8 fusion.41
  107.3 29.6 %all-reduce.2.cloned.1.call-done = f32[16,1024]{1,0:T(8,128)} async-done(((f32[16,1024]{1,0:T(8,128)}), f32[16,1024]{1,0:T(8,128)}) %all-reduce.2.cloned.1.call-update) | async-done | bytes 65552 | tf_op jit(solution)/shard_map/psum | solution.py:177
  136.9 1.0 multiply_reduce_fusion.1
  138.3 1.5 collective-permute-start.8
  139.8 2.4 %collective-permute-done.8 = bf16[16,1024]{1,0:T(8,128)(2,1)S(1)} collective-permute-done((bf16[16,1024]{1,0:T(8,128)(2,1)S(1)}, bf16[16,1024]{1,0:T(8,128)(2,1)S(1)}, u32[]{:S(2)}, u32[]{:S(2)}) %collective-permute-start.8) | collective-permute-done | bytes 32800 | tf_op jit(solution)/shard_map/ppermute | solution.py:16
  142.2 1.6 collective-permute-start.9
  143.8 6.4 %reshape.165 = bf16[16,64,16,64]{3,2,1,0:T(8,128)(2,1)} reshape(bf16[1,16,64,1024]{3,2,1,0:T(8,128)(2,1)} %param.30) | data formatting | bytes 4194304 | tf_op jit(solution)/shard_map/reshape | solution.py:185
  150.1 6.4 %reshape.166 = bf16[16,64,16,64]{3,2,1,0:T(8,128)(2,1)} reshape(bf16[1,16,64,1024]{3,2,1,0:T(8,128)(2,1)} %param.31) | data formatting | bytes 4194304 | tf_op jit(solution)/shard_map/reshape | solution.py:186
  156.8 4.7 %fusion.51 = (f32[4,16,16]{0,2,1:T(8,128)S(1)}, f32[4,16,16,64]{3,0,2,1:T(4,128)S(1)}) fusion(bf16[16,64,16,64]{3,2,1,0:T(8,128)(2,1)} %reshape.165, bf16[4,16,16,64]{3,2,1,0:T(8,128)(2,1)S(1)} %select_n.148), kind=kOutput, calls=%fused_computation.109 | convolution fusion | flops 8518656 | bytes 2494464 | tf_op jit(solution)/shard_map/bihe,iphe->bihp/dot_general | solution.py:188
  161.5 1.3 fusion.9
  162.8 0.9 all_gather_reshape.11
  163.9 0.7 fusion.23
  164.9 5.2 %all_gather.10 = f32[4,64,16]{1,2,0:T(8,128)S(1)} all-gather(f32[1,64,16]{1,2,0:T(8,128)S(1)} %all_gather_reshape.10), channel_id=1, replica_groups=mesh['dp'=8,'patch'=4] {'patch'}, dimensions={0}, use_global_device_ids=true | all-gather | bytes 20480 | tf_op jit(solution)/shard_map/all_gather | solution.py:20
  170.1 5.4 %all_gather.9 = f32[4,64,16]{1,2,0:T(8,128)S(1)} all-gather(f32[1,64,16]{1,2,0:T(8,128)S(1)} %all_gather_reshape.9), channel_id=1, replica_groups=mesh['dp'=8,'patch'=4] {'patch'}, dimensions={0}, use_global_device_ids=true | all-gather | bytes 20480 | tf_op jit(solution)/shard_map/all_gather | solution.py:20
  175.5 4.3 %all-gather.2.cloned.1.call-done = f32[4,64,1024]{2,1,0:T(8,128)} async-done(((f32[1,64,1024]{2,1,0:T(8,128)}), f32[4,64,1024]{2,1,0:T(8,128)}) %all-gather.2.cloned.1.call-update) | async-done | bytes 1048592 | tf_op jit(solution)/shard_map/all_gather | solution.py:20
  179.8 1.0 slice_bitcast_fusion
  180.8 6.1 %while.19 = (s32[]{:T(128)}, f32[64,16]{0,1:T(8,128)S(1)}, f32[64,16]{0,1:T(8,128)S(1)}, f32[64,1024]{1,0:T(8,128)S(1)}, f32[4,64,16]{1,2,0:T(8,128)S(1)}, /*ind...) while((s32[]{:T(128)}, f32[64,16]{0,1:T(8,128)S(1)}, ...), condition=%wide.region_11.12_spmd, body=%wide.region_10.11_spmd.sunk | while | flops 202757 | bytes 2941079 | solution.py:26
  181.8 1.1 fusion.67
  183.8 1.1 fusion.67
  185.8 1.1 fusion.67
  187.0 1.5 collective-permute-start.10
  188.6 0.5 collective-permute-start.14
  189.1 1.6 collective-permute-start.11
  190.7 1.6 collective-permute-done.14
  193.1 1.5 collective-permute-start.12
  194.7 0.6 collective-permute-start.15
  195.4 1.5 collective-permute-start.13
  196.9 1.5 collective-permute-done.15
  199.7 2.6 %fusion.19 = bf16[16,1024]{1,0:T(8,128)(2,1)} fusion(f32[16,1024]{1,0:T(8,128)S(1)} %get-tuple-element.210, bf16[1024,1024]{1,0:T(8,128)(2,1)} %param.29, f32[16,1024]{1,0:T(8,128)S(1)} %div.62, f32[16,1024]{1,0:T(8,128)S(1)} %collective-permute-done.13, f32[16,1024]{1,0:T(8,128)S(1)} %mul.400, f32[16,1024]{1,0:T(8,128)S(1)} %mul.397, ...), kind=kOutput, calls=%fused_computation.21 | convolution fusion | flops 33669120 | bytes 2523140 | tf_op jit(solution)/shard_map/dot_general | solution.py:212
  (146 shorter events, 12.2 us)
Async XLA Ops:
  7.2 130.7 %copy-start = (bf16[1024,1024]{1,0:T(8,128)(2,1)S(1)}, bf16[1024,1024]{1,0:T(8,128)(2,1)}, u32[]{:S(2)}) copy-start(bf16[1024,1024]{1,0:T(8,128)(2,1)} %param.28) | copy-start | bytes 6291460
  7.2 71.2 %reduce-scatter.2.cloned.1.call-start = ((), (), s32[]{:S(2)}) async-start(), calls=%async_computation.1 | async-start | bytes 589824 | tf_op jit(solution)/shard_map/reduce_scatter | solution.py:117
  7.2 5.7 %copy-start.8 = (bf16[1024]{0:T(1024)(128)(2,1)S(1)}, bf16[1024]{0:T(1024)(128)(2,1)}, u32[]{:S(2)}) copy-start(bf16[1024]{0:T(1024)(128)(2,1)} %param.20) | copy-start | bytes 6148
  7.3 73.0 %copy-start.5 = (bf16[1024,256]{1,0:T(8,128)(2,1)S(1)}, bf16[1024,256]{1,0:T(8,128)(2,1)}, u32[]{:S(2)}) copy-start(bf16[1024,256]{1,0:T(8,128)(2,1)} %param.21) | copy-start | bytes 1572868
  7.3 73.2 %copy-start.3 = (bf16[1024,256]{1,0:T(8,128)(2,1)S(1)}, bf16[1024,256]{1,0:T(8,128)(2,1)}, u32[]{:S(2)}) copy-start(bf16[1024,256]{1,0:T(8,128)(2,1)} %param.22) | copy-start | bytes 1572868
  7.3 74.8 %copy-start.10 = (s32[128]{0:T(128)S(1)}, s32[128]{0:T(128)}, u32[]{:S(2)}) copy-start(s32[128]{0:T(128)} %param.18) | copy-start | bytes 1540
  12.9 124.0 %all-reduce.2.cloned.1.call-start = ((), (), s32[]{:S(2)}) async-start(), calls=%async_computation.2 | async-start | bytes 131072 | tf_op jit(solution)/shard_map/psum | solution.py:177
  80.7 8.6 %copy-start.6 = (bf16[16,256]{1,0:T(8,128)(2,1)}, bf16[16,256]{1,0:T(8,128)(2,1)S(1)}, u32[]{:S(2)}) copy-start(bf16[16,256]{1,0:T(8,128)(2,1)S(1)} %get-tuple-element.230) | copy-start | bytes 24580
  80.7 5.5 %collective-permute-start = (bf16[2,16,256]{2,1,0:T(8,128)(2,1)S(1)}, bf16[2,16,256]{2,1,0:T(8,128)(2,1)S(1)}, u32[]{:S(2)}, u32[]{:S(2)}) collective-permute-start(bf16[2,16,256]{2,1,0:T(8,128)(2,1)S(1)} %pad_maximum_fusion), channel_id=1, source_target_pairs={{0,4},{4,0},{8,12},{12,8},{16,20},{20,16},{24,28},{28,24},{1,5},{5... | collective-permute-start | bytes 49160 | tf_op jit(solution)/shard_map/ppermute | solution.py:16
  86.2 21.1 %copy-start.9 = (bf16[1024]{0:T(1024)(128)(2,1)S(1)}, bf16[1024]{0:T(1024)(128)(2,1)}, u32[]{:S(2)}) copy-start(bf16[1024]{0:T(1024)(128)(2,1)} %param.27) | copy-start | bytes 6148
  86.2 50.7 %copy-start.2 = (f32[16,1024]{1,0:T(8,128)S(1)}, f32[16,1024]{1,0:T(8,128)}, u32[]{:S(2)}) copy-start(f32[16,1024]{1,0:T(8,128)} %reduce-scatter.2.cloned.1.call-done) | copy-start | bytes 196612
  86.2 4.0 %collective-permute-start.1 = (bf16[2,32,256]{2,1,0:T(8,128)(2,1)S(1)}, bf16[2,32,256]{2,1,0:T(8,128)(2,1)S(1)}, u32[]{:S(2)}, u32[]{:S(2)}) collective-permute-start(bf16[2,32,256]{2,1,0:T(8,128)(2,1)S(1)} %maximum_select_fusion.3), channel_id=1, source_target_pairs={{0,8},{4,12},{8,0},{12,4},{16,24},{20,28},{24,16},{28,20},{1,9},{5... | collective-permute-start | bytes 98312 | tf_op jit(solution)/shard_map/ppermute | solution.py:16
  89.0 49.3 %copy-start.7 = (bf16[16,256]{1,0:T(8,128)(2,1)}, bf16[16,256]{1,0:T(8,128)(2,1)S(1)}, u32[]{:S(2)}) copy-start(bf16[16,256]{1,0:T(8,128)(2,1)S(1)} %convolution_convert_fusion.1) | copy-start | bytes 24580
  90.8 15.4 %copy-start.4 = (bf16[256,1024]{1,0:T(8,128)(2,1)S(1)}, bf16[256,1024]{1,0:T(8,128)(2,1)}, u32[]{:S(2)}) copy-start(bf16[256,1024]{1,0:T(8,128)(2,1)} %param.24) | copy-start | bytes 1572868
  94.5 3.8 %collective-permute-start.2 = (f32[32,4]{1,0:T(8,128)S(1)}, f32[32,4]{1,0:T(8,128)S(1)}, u32[]{:S(2)}, u32[]{:S(2)}) collective-permute-start(f32[32,4]{1,0:T(8,128)S(1)} %constant_dynamic-slice_fusion.11), channel_id=1, source_target_pairs={{0,8},{4,12},{8,0},{12,4},{16,24},{20,28},{24,16},{28,20},{1,9},{5... | collective-permute-start | bytes 1544 | tf_op jit(solution)/shard_map/ppermute | solution.py:16
  96.1 3.7 %collective-permute-start.6 = (f32[32,4]{1,0:T(8,128)S(1)}, f32[32,4]{1,0:T(8,128)S(1)}, u32[]{:S(2)}, u32[]{:S(2)}) collective-permute-start(f32[32,4]{1,0:T(8,128)S(1)} %constant_dynamic-slice_fusion.7), channel_id=1, source_target_pairs={{0,8},{4,12},{8,0},{12,4},{16,24},{20,28},{24,16},{28,20},{1,9},{5... | collective-permute-start | bytes 1544 | tf_op jit(solution)/shard_map/ppermute | solution.py:16
  96.5 5.8 %collective-permute-start.3 = (f32[32,256]{1,0:T(8,128)S(1)}, f32[32,256]{1,0:T(8,128)S(1)}, u32[]{:S(2)}, u32[]{:S(2)}) collective-permute-start(f32[32,256]{1,0:T(8,128)S(1)} %constant_dynamic-slice_fusion.10), channel_id=1, source_target_pairs={{0,8},{4,12},{8,0},{12,4},{16,24},{20,28},{24,16},{28,20},{1,9},{5... | collective-permute-start | bytes 98312 | tf_op jit(solution)/shard_map/ppermute | solution.py:16
  100.2 3.7 %collective-permute-start.4 = (f32[16,4]{1,0:T(8,128)S(1)}, f32[16,4]{1,0:T(8,128)S(1)}, u32[]{:S(2)}, u32[]{:S(2)}) collective-permute-start(f32[16,4]{1,0:T(8,128)S(1)} %constant_dynamic-slice_fusion.9), channel_id=1, source_target_pairs={{0,4},{4,0},{8,12},{12,8},{16,20},{20,16},{24,28},{28,24},{1,5},{5... | collective-permute-start | bytes 776 | tf_op jit(solution)/shard_map/ppermute | solution.py:16
  100.8 3.7 %collective-permute-start.7 = (f32[16,4]{1,0:T(8,128)S(1)}, f32[16,4]{1,0:T(8,128)S(1)}, u32[]{:S(2)}, u32[]{:S(2)}) collective-permute-start(f32[16,4]{1,0:T(8,128)S(1)} %constant_dynamic-slice_fusion.6), channel_id=1, source_target_pairs={{0,4},{4,0},{8,12},{12,8},{16,20},{20,16},{24,28},{28,24},{1,5},{5... | collective-permute-start | bytes 776 | tf_op jit(solution)/shard_map/ppermute | solution.py:16
  102.4 3.8 %collective-permute-start.5 = (f32[16,256]{1,0:T(8,128)S(1)}, f32[16,256]{1,0:T(8,128)S(1)}, u32[]{:S(2)}, u32[]{:S(2)}) collective-permute-start(f32[16,256]{1,0:T(8,128)S(1)} %constant_dynamic-slice_fusion.8), channel_id=1, source_target_pairs={{0,4},{4,0},{8,12},{12,8},{16,20},{20,16},{24,28},{28,24},{1,5},{5... | collective-permute-start | bytes 49160 | tf_op jit(solution)/shard_map/ppermute | solution.py:16
  107.0 72.8 %all-gather.2.cloned.1.call-start = ((), (), s32[]{:S(2)}) async-start(), calls=%async_computation.3 | async-start | bytes 1310720 | tf_op jit(solution)/shard_map/all_gather | solution.py:20
  138.3 3.9 %collective-permute-start.8 = (bf16[16,1024]{1,0:T(8,128)(2,1)S(1)}, bf16[16,1024]{1,0:T(8,128)(2,1)S(1)}, u32[]{:S(2)}, u32[]{:S(2)}) collective-permute-start(bf16[16,1024]{1,0:T(8,128)(2,1)S(1)} %convolution_convert_fusion), channel_id=1, source_target_pairs={{0,4},{4,0},{8,12},{12,8},{16,20},{20,16},{24,28},{28,24},{1,5},{5... | collective-permute-start | bytes 98312 | tf_op jit(solution)/shard_map/ppermute | solution.py:16
  142.2 14.3 %collective-permute-start.9 = (bf16[32,1024]{1,0:T(8,128)(2,1)S(1)}, bf16[32,1024]{1,0:T(8,128)(2,1)S(1)}, u32[]{:S(2)}, u32[]{:S(2)}) collective-permute-start(bf16[32,1024]{1,0:T(8,128)(2,1)S(1)} %maximum_select_fusion.2), channel_id=1, source_target_pairs={{0,8},{4,12},{8,0},{12,4},{16,24},{20,28},{24,16},{28,20},{1,9},{5... | collective-permute-start | bytes 196616 | tf_op jit(solution)/shard_map/ppermute | solution.py:16
  156.8 4.7 %copy-start.1 = (bf16[16,64,16,64]{3,2,1,0:T(8,128)(2,1)S(1)}, bf16[16,64,16,64]{3,2,1,0:T(8,128)(2,1)}, u32[]{:S(2)}) copy-start(bf16[16,64,16,64]{3,2,1,0:T(8,128)(2,1)} %reshape.166) | copy-start | bytes 6291460
  187.0 3.7 %collective-permute-start.10 = (f32[32,16]{0,1:T(8,128)S(1)}, f32[32,16]{0,1:T(8,128)S(1)}, u32[]{:S(2)}, u32[]{:S(2)}) collective-permute-start(f32[32,16]{0,1:T(8,128)S(1)} %constant_dynamic-slice_fusion.5), channel_id=1, source_target_pairs={{0,8},{4,12},{8,0},{12,4},{16,24},{20,28},{24,16},{28,20},{1,9},{5... | collective-permute-start | bytes 6152 | tf_op jit(solution)/shard_map/ppermute | solution.py:16
  188.6 3.7 %collective-permute-start.14 = (f32[32,16]{0,1:T(8,128)S(1)}, f32[32,16]{0,1:T(8,128)S(1)}, u32[]{:S(2)}, u32[]{:S(2)}) collective-permute-start(f32[32,16]{0,1:T(8,128)S(1)} %constant_dynamic-slice_fusion.1), channel_id=1, source_target_pairs={{0,8},{4,12},{8,0},{12,4},{16,24},{20,28},{24,16},{28,20},{1,9},{5... | collective-permute-start | bytes 6152 | tf_op jit(solution)/shard_map/ppermute | solution.py:16
  189.1 6.2 %collective-permute-start.11 = (f32[32,1024]{1,0:T(8,128)S(1)}, f32[32,1024]{1,0:T(8,128)S(1)}, u32[]{:S(2)}, u32[]{:S(2)}) collective-permute-start(f32[32,1024]{1,0:T(8,128)S(1)} %constant_dynamic-slice_fusion.4), channel_id=1, source_target_pairs={{0,8},{4,12},{8,0},{12,4},{16,24},{20,28},{24,16},{28,20},{1,9},{5... | collective-permute-start | bytes 393224 | tf_op jit(solution)/shard_map/ppermute | solution.py:16
  193.1 3.8 %collective-permute-start.12 = (f32[16,16]{0,1:T(8,128)S(1)}, f32[16,16]{0,1:T(8,128)S(1)}, u32[]{:S(2)}, u32[]{:S(2)}) collective-permute-start(f32[16,16]{0,1:T(8,128)S(1)} %constant_dynamic-slice_fusion.3), channel_id=1, source_target_pairs={{0,4},{4,0},{8,12},{12,8},{16,20},{20,16},{24,28},{28,24},{1,5},{5... | collective-permute-start | bytes 3080 | tf_op jit(solution)/shard_map/ppermute | solution.py:16
  194.7 3.7 %collective-permute-start.15 = (f32[16,16]{0,1:T(8,128)S(1)}, f32[16,16]{0,1:T(8,128)S(1)}, u32[]{:S(2)}, u32[]{:S(2)}) collective-permute-start(f32[16,16]{0,1:T(8,128)S(1)} %constant_dynamic-slice_fusion), channel_id=1, source_target_pairs={{0,4},{4,0},{8,12},{12,8},{16,20},{20,16},{24,28},{28,24},{1,5},{5... | collective-permute-start | bytes 3080 | tf_op jit(solution)/shard_map/ppermute | solution.py:16
  195.4 4.3 %collective-permute-start.13 = (f32[16,1024]{1,0:T(8,128)S(1)}, f32[16,1024]{1,0:T(8,128)S(1)}, u32[]{:S(2)}, u32[]{:S(2)}) collective-permute-start(f32[16,1024]{1,0:T(8,128)S(1)} %constant_dynamic-slice_fusion.2), channel_id=1, source_target_pairs={{0,4},{4,0},{8,12},{12,8},{16,20},{20,16},{24,28},{28,24},{1,5},{5... | collective-permute-start | bytes 196616 | tf_op jit(solution)/shard_map/ppermute | solution.py:16
Sparse Core Ops, SparseCore 0:
  13.0 65.3 reduce-scatter.1
  107.1 29.7 all-reduce.1
  163.8 15.9 all-gather.1
where the time goes:
time: 210 us; the launch traced here: 209 us
  waiting for transfers between devices  111 us (53%)
  local copies, waits for them, and re-layouts  26.4 us (13%)
  starting transfers between devices  19.8 us (9%)
  matrix products  19.4 us (9%)
  between operations  14.2 us (7%)
  blocking collectives  10.6 us (5%)
  other arithmetic  7.84 us (4%)
    reduce_scatter x1, waiting for transfers between devices, shards(): lax.psum_scatter(jnp.dot(onehot_table, embedding, preferred_element_type=...  65.4 us
    psum x1, waiting for transfers between devices, shards(): lax.psum(jnp.dot(self_context, output_weight, preferred_element_type=jnp....  29.6 us
    ppermute x16, starting transfers between devices, from_partner(): return lax.ppermute(value, axis, pairs)  19.5 us
    ppermute x16, waiting for transfers between devices, from_partner(): return lax.ppermute(value, axis, pairs)  11.2 us
    all_gather x2, blocking collectives, joined(): everything = jax.tree.map(lambda part: lax.all_gather(part, axis), x)  10.6 us
    reshape x1, local copies, waits for them, and re-layouts, shards(): image_values.reshape(row_count, patch_count, HEADS, head_size)  6.4 us
    reshape x1, local copies, waits for them, and re-layouts, shards(): patch_keys = image_keys.reshape(row_count, patch_count, HEADS, head_size)  6.37 us
    dot_general x1, matrix products, shards(): jnp.dot(onehot_table, embedding, preferred_element_type=jnp.float32)  5.58 us
  transfers between devices with their start and end apart: 19, of which 13 were waited for; matrix products, arithmetic and copies ran while one was open for 11% of the time, Pallas kernels for 0%

commit v1 on v0

v1 whole, which is shorter than its diff:
```python
import functools
import math

import jax
import jax.numpy as jnp
from jax import lax
from jax.experimental import pallas as pl
from jax.experimental.pallas import tpu as pltpu
from jax.sharding import PartitionSpec as P

HEADS = 16
BEAMS = 4
SUB = 8
PAIR = SUB // BEAMS
LANES = 128
LOW = -1e30

f32 = jnp.float32
bf16 = jnp.bfloat16


def swap(value, axis, mask):
    pairs = [(source, source ^ mask) for source in range(lax.axis_size(axis))]
    return lax.ppermute(value, axis, pairs)


def params(mib):
    return pltpu.CompilerParams(vmem_limit_bytes=mib * 2**20)


def dot(a, b):
    return jnp.dot(a, b, preferred_element_type=f32)


def dot_nt(a, b):
    return lax.dot_general(a, b, (((1,), (1,)), ((), ())), preferred_element_type=f32)


def normalize(inputs, gains):
    factor = lax.rsqrt(jnp.mean(inputs * inputs, axis=-1, keepdims=True) + 1e-06)
    return (inputs * factor * gains.astype(f32)).astype(bf16)


def place():
    position = lax.axis_index("dp")
    return position // BEAMS, position % BEAMS, lax.axis_index("patch") % 2


def join_halves(own_ref, other_ref, core):
    own = own_ref[...].astype(f32)
    other = other_ref[...].astype(f32)
    return jnp.concatenate([jnp.where(core == 0, own, other), jnp.where(core == 0, other, own)], 0)


def gather_kernel(ids_ref, table_ref, *refs, groups, images, slab):
    outs, (blocks, sem) = refs[:-2], refs[-2:]
    group, _, core = place()
    first = lax.axis_index("dp") * slab
    here = images // 2
    rows = here * BEAMS
    width = blocks.shape[2]

    def local_id(k):
        slot, rest = k // rows, k % rows
        row = ((group ^ slot) * BEAMS + rest % BEAMS) * images + core * here + rest // BEAMS
        return ids_ref[row] - first

    def start(k, carry):
        held = jnp.clip(local_id(k), 0, slab - 1)
        pltpu.make_async_copy(table_ref.at[held // SUB], blocks.at[k], sem).start()
        return carry

    lax.fori_loop(0, groups * rows, start, 0, unroll=SUB)
    pltpu.make_async_copy(blocks, blocks, sem).wait()
    sub = lax.broadcasted_iota(jnp.int32, (SUB, width), 0)
    for slot in range(groups):
        for base in range(0, rows, 2 * SUB):
            tiles = []
            for tile in (base, base + SUB):
                packed = jnp.zeros((SUB, width), f32)
                for k in range(SUB):
                    at = slot * rows + tile + k
                    local = local_id(at)
                    mine = jnp.logical_and(local >= 0, local < slab)
                    place_in = jnp.clip(local, 0, slab - 1) % SUB
                    turned = pltpu.roll(blocks[at].astype(f32), (k + SUB - place_in) % SUB, 0)
                    packed = jnp.where(jnp.logical_and(sub == k, mine), turned, packed)
                tiles.append(packed)
            outs[slot][base : base + 2 * SUB, :] = jnp.concatenate(tiles, 0).astype(bf16)


def spread(rows8, heads, head_size):
    owner = lax.broadcasted_iota(jnp.int32, rows8.shape, 1) // head_size
    return jnp.concatenate([jnp.where(owner == h, rows8, 0.0) for h in range(heads)], 0)


def fold(wide, heads, head_size):
    owner = lax.broadcasted_iota(jnp.int32, (SUB, wide.shape[1]), 1) // head_size
    folded = wide[:SUB]
    for h in range(1, heads):
        folded = jnp.where(owner == h, wide[h * SUB : (h + 1) * SUB], folded)
    return folded


def same_image(shape, length):
    row = lax.broadcasted_iota(jnp.int32, shape, 0) % SUB // BEAMS
    return row == lax.broadcasted_iota(jnp.int32, shape, 1) // length


def self_kernel(parents_ref, own_ref, other_ref, gain_ref, wq_ref, wk_ref, wv_ref, pk_ref, pv_ref,
                context_ref, key_ref, value_ref, key_scr, value_scr, *, head_size):
    group, beam, core = place()
    images, length, width = pk_ref.shape
    heads = width // head_size
    scaling = 1.0 / math.sqrt(head_size)
    normed = normalize(join_halves(own_ref, other_ref, core), gain_ref[...])
    queries = dot(normed, wq_ref[...]).astype(bf16).astype(f32)
    keys = dot(normed, wk_ref[...]).astype(bf16).astype(f32)
    values = dot(normed, wv_ref[...]).astype(bf16).astype(f32)
    for first in range(0, width, LANES):
        key_scr[first // LANES] = keys[:, first : first + LANES]
        value_scr[first // LANES] = values[:, first : first + LANES]
    for first in range(0, width, LANES):
        mine = pl.ds(beam, images, stride=BEAMS)
        key_ref[:, first : first + LANES] = key_scr[first // LANES, mine, :].astype(bf16)
        value_ref[:, first : first + LANES] = value_scr[first // LANES, mine, :].astype(bf16)
    sub = lax.broadcasted_iota(jnp.int32, (SUB, width), 0)
    pairs = images // PAIR
    seen = same_image((heads * SUB, PAIR * length), length)
    scores, owns = [], []
    for j in range(pairs):
        q = spread(queries[j * SUB : (j + 1) * SUB], heads, head_size)
        k = jnp.concatenate([keys[j * SUB : (j + 1) * SUB]] * heads, 0)
        past = pk_ref[j * PAIR : (j + 1) * PAIR].reshape(PAIR * length, width)
        scores.append(dot_nt(q.astype(bf16), past))
        owns.append(jnp.sum(q * k, axis=-1, keepdims=True) * scaling)
    weights, own_weights, totals = [], [], []
    for j in range(pairs):
        s = jnp.where(seen, scores[j] * scaling, LOW)
        peak = jnp.maximum(jnp.max(s, axis=-1, keepdims=True), owns[j])
        power = jnp.exp(s - peak)
        own_power = jnp.exp(owns[j] - peak)
        totals.append(jnp.sum(power, axis=-1, keepdims=True) + own_power)
        weights.append(power.astype(bf16))
        own_weights.append(own_power.astype(bf16).astype(f32))
    done = []
    for j in range(pairs):
        past = pv_ref[j * PAIR : (j + 1) * PAIR].reshape(PAIR * length, width)
        v = jnp.concatenate([values[j * SUB : (j + 1) * SUB]] * heads, 0)
        summed = (dot(weights[j], past) + own_weights[j] * v) / totals[j]
        folded = fold(summed, heads, head_size)
        lives = jnp.zeros((SUB, width), jnp.int32)
        for k in range(SUB):
            row = (group * BEAMS + k % BEAMS) * images + j * PAIR + k // BEAMS
            lives = jnp.where(sub == k, (parents_ref[row] == beam).astype(jnp.int32), lives)
        done.append(jnp.where(lives > 0, folded, 0.0))
    context_ref[...] = jnp.concatenate(done, 0).astype(bf16)


def cross_kernel(*refs, pieces, head_size):
    contexts = refs[:pieces]
    outputs = refs[pieces : 2 * pieces]
    own_ref, other_ref, gain_ref, query_ref, ik_ref, iv_ref = refs[2 * pieces : 2 * pieces + 6]
    middle_ref, *messages = refs[2 * pieces + 6 : 2 * pieces + 7 + BEAMS]
    mid_scr, sum_scr, s_scr, p_scr = refs[2 * pieces + 7 + BEAMS :]
    _, beam, core = place()
    _, images, length, width = ik_ref.shape
    scaling = 1.0 / math.sqrt(head_size)
    middle = join_halves(own_ref, other_ref, core)
    for piece in range(pieces):
        middle = middle + dot(contexts[piece][...], outputs[piece][...])
    mine = pl.ds(beam, images, stride=BEAMS)
    for first in range(0, width, LANES):
        mid_scr[first // LANES] = middle[:, first : first + LANES]
    for first in range(0, width, LANES):
        middle_ref[:, first : first + LANES] = mid_scr[first // LANES, mine, :]
    probes = dot(normalize(middle, gain_ref[...]), query_ref[...]).astype(bf16).astype(f32)
    pairs = images // PAIR
    block = min(width, 2 * LANES)
    heads = block // head_size
    blocks = width // block
    rows = heads * SUB
    for j in range(pairs):
        for n in range(blocks):
            at = slice(n * block, (n + 1) * block)
            q = spread(probes[j * SUB : (j + 1) * SUB, at], heads, head_size).astype(bf16)
            past = ik_ref[0, j * PAIR : (j + 1) * PAIR, :, at].reshape(PAIR * length, block)
            s_scr[(j * blocks + n) * rows : (j * blocks + n + 1) * rows, :] = dot_nt(q, past)
    seen = same_image((rows, PAIR * length), length)
    lane = lax.broadcasted_iota(jnp.int32, (SUB, LANES), 1)
    for j in range(pairs):
        stats = jnp.zeros((SUB, LANES), f32)
        for n in range(blocks):
            at = slice((j * blocks + n) * rows, (j * blocks + n + 1) * rows)
            s = jnp.where(seen, s_scr[at, :] * scaling, LOW)
            peak = jnp.max(s, axis=-1, keepdims=True)
            power = jnp.exp(s - peak)
            total = jnp.sum(power, axis=-1, keepdims=True)
            p_scr[at, :] = power.astype(bf16)
            for h in range(heads):
                head = n * heads + h
                stats = jnp.where(lane == head, peak[h * SUB : (h + 1) * SUB], stats)
                stats = jnp.where(lane == HEADS + head, total[h * SUB : (h + 1) * SUB], stats)
        sum_scr[width // LANES, j * SUB : (j + 1) * SUB, :] = stats
    for j in range(pairs):
        for n in range(blocks):
            at = slice((j * blocks + n) * rows, (j * blocks + n + 1) * rows)
            past = iv_ref[0, j * PAIR : (j + 1) * PAIR, :, n * block : (n + 1) * block]
            summed = fold(dot(p_scr[at, :], past.reshape(PAIR * length, block)), heads, head_size)
            for part in range(block // LANES):
                sum_scr[n * (block // LANES) + part, j * SUB : (j + 1) * SUB, :] = summed[
                    :, part * LANES : (part + 1) * LANES
                ]
    for k in range(BEAMS):
        theirs = pl.ds(beam ^ k, images, stride=BEAMS)
        for part in range(width // LANES + 1):
            messages[k][:, part * LANES : (part + 1) * LANES] = sum_scr[part, theirs, :]


def merge(parts, head_size):
    width = parts[0].shape[1] - LANES
    lane = lax.broadcasted_iota(jnp.int32, (1, LANES), 1)
    stats = [part[:, width:] for part in parts]
    peak = functools.reduce(jnp.maximum, stats)
    row = lax.broadcasted_iota(jnp.int32, (LANES, width), 0)
    owner = lax.broadcasted_iota(jnp.int32, (LANES, width), 1) // head_size
    widen = (row == owner).astype(f32)
    total = 0.0
    sums = 0.0
    for part, stat in zip(parts, stats):
        scale = jnp.where(lane < HEADS, jnp.exp(stat - peak), 0.0)
        total = total + pltpu.roll(stat, LANES - HEADS, 1) * scale
        sums = sums + part[:, :width] * jnp.dot(scale, widen, precision=lax.Precision.HIGHEST)
    return sums, peak, total, lane, widen


def merge_kernel(*refs, head_size):
    parts, out_ref = [ref[...] for ref in refs[:-1]], refs[-1]
    sums, peak, total, lane, _ = merge(parts, head_size)
    width = sums.shape[1]
    out_ref[:, :width] = sums
    out_ref[:, width:] = jnp.where(lane < HEADS, peak, pltpu.roll(total, HEADS, 1))


def final_kernel(*refs, head_size):
    parts = [ref[...] for ref in refs[:-3]]
    middle_ref, weight_ref, out_ref = refs[-3:]
    sums, _, total, lane, widen = merge(parts, head_size)
    total = jnp.where(lane < HEADS, total, 1.0)
    wide = jnp.dot(total, widen, precision=lax.Precision.HIGHEST)
    context = (sums / wide).astype(bf16)
    out_ref[...] = (middle_ref[...] + dot(context, weight_ref[...])).astype(bf16)


def shards(
    token_ids,
    parents,
    embedding,
    self_gain,
    query_weight,
    key_weight,
    value_weight,
    output_weight,
    past_keys,
    past_values,
    cross_gain,
    cross_query,
    cross_output,
    image_keys,
    image_values,
):
    images, length, width_here = past_keys.shape
    slab, width = embedding.shape
    head_size = width // HEADS
    groups = lax.axis_size("dp") // BEAMS
    patches = lax.axis_size("patch")
    group_rows = BEAMS * images
    half = group_rows // 2
    smem = pl.BlockSpec(memory_space=pltpu.SMEM)
    vmem = pl.BlockSpec(memory_space=pltpu.VMEM)

    outputs = [output_weight]
    mask = 1
    while mask < patches:
        outputs = outputs + [swap(piece, "patch", mask) for piece in outputs]
        mask *= 2

    slots = pl.pallas_call(
        functools.partial(gather_kernel, groups=groups, images=images, slab=slab),
        out_shape=[jax.ShapeDtypeStruct((half, width), bf16)] * groups,
        in_specs=[smem, pl.BlockSpec(memory_space=pl.ANY)],
        out_specs=[vmem] * groups,
        scratch_shapes=[
            pltpu.VMEM((groups * half, SUB, width), bf16),
            pltpu.SemaphoreType.DMA,
        ],
        compiler_params=params(16),
        name="gather",
    )(token_ids, embedding.reshape(slab // SUB, SUB, width))
    while len(slots) > 1:
        keep = len(slots) // 2
        slots = [a + swap(b, "dp", keep * BEAMS) for a, b in zip(slots[:keep], slots[keep:])]
    own = slots[0]
    own = own + swap(own, "dp", 1) + swap(own, "dp", 2) + swap(own, "dp", 3)
    other = swap(own, "patch", 1)

    context, new_key, new_value = pl.pallas_call(
        functools.partial(self_kernel, head_size=head_size),
        out_shape=[
            jax.ShapeDtypeStruct((group_rows, width_here), bf16),
            jax.ShapeDtypeStruct((images, width_here), bf16),
            jax.ShapeDtypeStruct((images, width_here), bf16),
        ],
        in_specs=[smem] + [vmem] * 8,
        out_specs=[vmem] * 3,
        scratch_shapes=[pltpu.VMEM((width_here // LANES, group_rows, LANES), f32)] * 2,
        compiler_params=params(16),
        name="self_attention",
    )(parents, own, other, self_gain.reshape(1, width), query_weight, key_weight, value_weight,
      past_keys, past_values)
    context = context + swap(context, "dp", 1) + swap(context, "dp", 2) + swap(context, "dp", 3)
    contexts = [context] + [swap(context, "patch", k) for k in range(1, patches)]

    patch_count = image_keys.shape[2]
    score_rows = images // PAIR * HEADS * SUB
    middle, *messages = pl.pallas_call(
        functools.partial(cross_kernel, pieces=patches, head_size=head_size),
        out_shape=[jax.ShapeDtypeStruct((images, width), f32)]
        + [jax.ShapeDtypeStruct((images, width + LANES), f32)] * BEAMS,
        in_specs=[vmem] * (2 * patches + 6),
        out_specs=[vmem] * (1 + BEAMS),
        scratch_shapes=[
            pltpu.VMEM((width // LANES, group_rows, LANES), f32),
            pltpu.VMEM((width // LANES + 1, group_rows, LANES), f32),
            pltpu.VMEM((score_rows, PAIR * patch_count), f32),
            pltpu.VMEM((score_rows, PAIR * patch_count), bf16),
        ],
        compiler_params=params(24),
        name="cross_attention",
    )(*contexts, *outputs, own, other, cross_gain.reshape(1, width), cross_query, image_keys,
      image_values)
    parts = [messages[0]] + [swap(messages[k], "dp", k) for k in range(1, BEAMS)]
    part = pl.pallas_call(
        functools.partial(merge_kernel, head_size=head_size),
        out_shape=jax.ShapeDtypeStruct((images, width + LANES), f32),
        in_specs=[vmem] * BEAMS,
        out_specs=vmem,
        compiler_params=params(8),
        name="merge",
    )(*parts)
    parts = [part] + [swap(part, "patch", k) for k in range(1, patches)]
    hidden = pl.pallas_call(
        functools.partial(final_kernel, head_size=head_size),
        out_shape=jax.ShapeDtypeStruct((images, width), bf16),
        in_specs=[vmem] * (patches + 2),
        out_specs=vmem,
        compiler_params=params(8),
        name="final",
    )(*parts, middle, cross_output)
    return (hidden, new_key, new_value)


def solution(mesh):
    in_specs = (
        P(),
        P(),
        P("dp", None),
        P(),
        P(None, "patch"),
        P(None, "patch"),
        P(None, "patch"),
        P("patch", None),
        P("dp", None, "patch"),
        P("dp", None, "patch"),
        P(),
        P(),
        P(),
        P("dp", None, "patch", None),
        P("dp", None, "patch", None),
    )
    out_specs = (P("dp", None), P("dp", "patch"), P("dp", "patch"))
    return jax.shard_map(shards, mesh=mesh, in_specs=in_specs, out_specs=out_specs, check_vma=False)
```

time: 210 us -> 64.8 us (0.31)
  waiting for transfers between devices: 111 us -> 28.4 us
  local copies, waits for them, and re-layouts: 26.4 us -> 4.05 us
  matrix products: 19.4 us -> 0 us
  between operations: 14.2 us -> 0.85 us
  blocking collectives: 10.6 us -> 0 us
  Pallas kernels: 0 us -> 10.5 us
  other arithmetic: 7.84 us -> 0.05 us
    reduce_scatter x1 -> x0, waiting for transfers between devices: 65.4 us -> none  [shards(): lax.psum_scatter(jnp.dot(onehot_table, embedding, preferred_element_type=...]
    psum x1 -> x0, waiting for transfers between devices: 29.6 us -> none  [shards(): lax.psum(jnp.dot(self_context, output_weight, preferred_element_type=jnp....]
    dot_general x11 -> x0, matrix products: 19.4 us -> none  [the longest x1 5.58 us: shards(): jnp.dot(onehot_table, embedding, preferred_element_type=jnp.float32)]
    ppermute x16 -> x20, waiting for transfers between devices: 11.2 us -> 28.4 us  [swap(): return lax.ppermute(value, axis, pairs)]
    reshape x3 -> x2, local copies, waits for them, and re-layouts: 12.9 us -> 0.01 us  [the longest x1 0.01 us: shards(): self_gain.reshape(1, width)]
    all_gather x2 -> x0, blocking collectives: 10.6 us -> none  [joined(): everything = jax.tree.map(lambda part: lax.all_gather(part, axis), x)]
    pallas_call x0 -> x5, Pallas kernels: none -> 10.5 us  [the longest x1 3.99 us: shards(): pl.pallas_call(functools.partial(gather_kernel, groups=groups, images=ima...]
    all_gather x1 -> x0, waiting for transfers between devices: 4.29 us -> none  [joined(): everything = jax.tree.map(lambda part: lax.all_gather(part, axis), x)]
  transfers between devices with their start and end apart: 19 -> 20, of which waited for: 13 -> 13; matrix products, arithmetic and copies ran while one was open for 11% -> 0% of each run, Pallas kernels for 0% -> 9%
where the time goes in v1:
time: 64.8 us; the launch traced here: 64.7 us
  waiting for transfers between devices  28.4 us (44%)
  starting transfers between devices  20.7 us (32%)
  Pallas kernels  10.5 us (16%)
  local copies, waits for them, and re-layouts  4.05 us (6%)
  between operations  0.85 us (1%)
    ppermute x20, waiting for transfers between devices, swap(): return lax.ppermute(value, axis, pairs)  28.4 us
    ppermute x20, starting transfers between devices, swap(): return lax.ppermute(value, axis, pairs)  20.7 us
    unnamed x30, local copies, waits for them, and re-layouts  4.04 us
    pallas_call x1, Pallas kernels, shards(): pl.pallas_call(functools.partial(gather_kernel, groups=groups, images=ima...  3.99 us
    pallas_call x1, Pallas kernels, shards(): pl.pallas_call(functools.partial(cross_kernel, pieces=patches, head_size=...  2.12 us
    pallas_call x1, Pallas kernels, shards(): pl.pallas_call(functools.partial(self_kernel, head_size=head_size), out_s...  2.05 us
    pallas_call x1, Pallas kernels, shards(): pl.pallas_call(functools.partial(final_kernel, head_size=head_size), out_...  1.73 us
  transfers between devices with their start and end apart: 20, of which 13 were waited for; matrix products, arithmetic and copies ran while one was open for 0% of the time, Pallas kernels for 9%

profile of v1, /device:TPU:0, one launch (start us, length us, event | category | flops | bytes accessed | tf_op | source)
XLA Modules:
  0.0 64.7 jit_solution(8727603944371214317)
XLA Ops:
  0.6 0.6 collective-permute-start.11
  1.2 3.3 %copy-done = bf16[4000,1024]{1,0:T(8,128)(2,1)S(1)} copy-done((bf16[4000,1024]{1,0:T(8,128)(2,1)S(1)}, bf16[4000,1024]{1,0:T(8,128)(2,1)}, u32[]{:S(2)}) %copy-start) | copy-done | bytes 8192024
  4.5 0.7 %copy-done.11 = s32[128]{0:T(128)S(1)} copy-done((s32[128]{0:T(128)S(1)}, s32[128]{0:T(128)}, u32[]{:S(2)}) %copy-start.11) | copy-done | bytes 536
  5.2 0.0 copy-start.4
  5.2 4.0 %gather.1 = (bf16[32,1024]{1,0:T(8,128)(2,1)S(1)}, bf16[32,1024]{1,0:T(8,128)(2,1)S(1)}) custom-call(s32[128]{0:T(128)S(1)} %copy-done.11, bf16[500,8,1024]{2,1,0:T(8,128)(2,1)S(1)} %bitcast.1), custom_call_target="tpu_custom_call" | custom-call | tf_op jit(solution)/shard_map/gather/pallas_call | solution.py:288
  9.2 3.7 %collective-permute-start = (bf16[32,1024]{1,0:T(8,128)(2,1)S(1)}, bf16[32,1024]{1,0:T(8,128)(2,1)S(1)}, u32[]{:S(2)}, u32[]{:S(2)}) collective-permute-start(bf16[32,1024]{1,0:T(8,128)(2,1)S(1)} %get-tuple-element.14), channel_id=1, source_target_pairs={{0,16},{4,20},{8,24},{12,28},{16,0},{20,4},{24,8},{28,12},{1,17},{... | collective-permute-start | bytes 196616 | tf_op jit(solution)/shard_map/ppermute | solution.py:24
  12.9 4.2 %collective-permute-done = bf16[32,1024]{1,0:T(8,128)(2,1)S(1)} collective-permute-done((bf16[32,1024]{1,0:T(8,128)(2,1)S(1)}, bf16[32,1024]{1,0:T(8,128)(2,1)S(1)}, u32[]{:S(2)}, u32[]{:S(2)}) %collective-permute-start) | collective-permute-done | bytes 65568 | tf_op jit(solution)/shard_map/ppermute | solution.py:24
  17.1 0.0 copy-start.14
  17.1 0.0 copy-start.2
  17.1 0.0 copy-start.3
  17.1 1.7 %collective-permute-start.3 = (bf16[32,1024]{1,0:T(8,128)(2,1)S(1)}, bf16[32,1024]{1,0:T(8,128)(2,1)S(1)}, u32[]{:S(2)}, u32[]{:S(2)}) collective-permute-start(bf16[32,1024]{1,0:T(8,128)(2,1)S(1)} %add.21), channel_id=1, source_target_pairs={{0,12},{4,8},{8,4},{12,0},{16,28},{20,24},{24,20},{28,16},{1,13},{... | collective-permute-start | bytes 196616 | tf_op jit(solution)/shard_map/ppermute | solution.py:24
  18.8 1.3 %collective-permute-start.2 = (bf16[32,1024]{1,0:T(8,128)(2,1)S(1)}, bf16[32,1024]{1,0:T(8,128)(2,1)S(1)}, u32[]{:S(2)}, u32[]{:S(2)}) collective-permute-start(bf16[32,1024]{1,0:T(8,128)(2,1)S(1)} %add.21), channel_id=1, source_target_pairs={{0,8},{4,12},{8,0},{12,4},{16,24},{20,28},{24,16},{28,20},{1,9},{5... | collective-permute-start | bytes 196616 | tf_op jit(solution)/shard_map/ppermute | solution.py:24
  20.2 0.5 collective-permute-start.1
  20.7 1.6 %collective-permute-start.12 = (bf16[256,1024]{1,0:T(8,128)(2,1)S(1)}, bf16[256,1024]{1,0:T(8,128)(2,1)S(1)}, u32[]{:S(2)}, u32[]{:S(2)}) collective-permute-start(bf16[256,1024]{1,0:T(8,128)(2,1)S(1)} %copy-done.10), channel_id=1, source_target_pairs={{0,2},{1,3},{2,0},{3,1},{4,6},{5,7},{6,4},{7,5},{8,10},{9,11},{10,... | collective-permute-start | bytes 1572872 | tf_op jit(solution)/shard_map/ppermute | solution.py:24
  22.2 0.0 collective-permute-done.11.refs_5_
  22.2 0.5 collective-permute-start.13
  22.7 0.0 collective-permute-done.3
  22.7 0.6 collective-permute-done.2
  23.3 1.1 %collective-permute-done.1 = bf16[32,1024]{1,0:T(8,128)(2,1)S(1)} collective-permute-done((bf16[32,1024]{1,0:T(8,128)(2,1)S(1)}, bf16[32,1024]{1,0:T(8,128)(2,1)S(1)}, u32[]{:S(2)}, u32[]{:S(2)}) %collective-permute-start.1) | collective-permute-done | bytes 65568 | tf_op jit(solution)/shard_map/ppermute | solution.py:24
  24.5 0.1 collective-permute-start.4
  24.6 1.2 %collective-permute-done.4.other_ref.refs_9_ = bf16[32,1024]{1,0:T(8,128)(2,1)S(1)} collective-permute-done((bf16[32,1024]{1,0:T(8,128)(2,1)S(1)}, bf16[32,1024]{1,0:T(8,128)(2,1)S(1)}, u32[]{:S(2)}, u32[]{:S(2)}) %collective-permute-start.4) | collective-permute-done | bytes 65568 | tf_op jit(solution)/shard_map/ppermute | solution.py:24
  25.8 2.1 %self_attention.1 = (bf16[64,256]{1,0:T(8,128)(2,1)S(1)}, bf16[16,256]{1,0:T(8,128)(2,1)}, bf16[16,256]{1,0:T(8,128)(2,1)}) custom-call(s32[128]{0:T(128)S(1)} %copy-done.12, bf16[32,1024]{1,0:T(8,128)(2,1)S(1)} %add_add_fusion.own_ref.refs_8_, bf16[32,1024]{1,0:T(8,128)(2,1)S(1)} %collective-permute-done.4.other_ref.refs_9_, ...), custom_call_target="tpu_custom_call" | custom-call | tf_op jit(solution)/shard_map/self_attention/pallas_call | solution.py:307
  27.9 0.8 %collective-permute-start.7 = (bf16[64,256]{1,0:T(8,128)(2,1)S(1)}, bf16[64,256]{1,0:T(8,128)(2,1)S(1)}, u32[]{:S(2)}, u32[]{:S(2)}) collective-permute-start(bf16[64,256]{1,0:T(8,128)(2,1)S(1)} %get-tuple-element.15), channel_id=1, source_target_pairs={{0,12},{4,8},{8,4},{12,0},{16,28},{20,24},{24,20},{28,16},{1,13},{... | collective-permute-start | bytes 98312 | tf_op jit(solution)/shard_map/ppermute | solution.py:24
  28.6 1.2 %collective-permute-start.6 = (bf16[64,256]{1,0:T(8,128)(2,1)S(1)}, bf16[64,256]{1,0:T(8,128)(2,1)S(1)}, u32[]{:S(2)}, u32[]{:S(2)}) collective-permute-start(bf16[64,256]{1,0:T(8,128)(2,1)S(1)} %get-tuple-element.15), channel_id=1, source_target_pairs={{0,8},{4,12},{8,0},{12,4},{16,24},{20,28},{24,16},{28,20},{1,9},{5... | collective-permute-start | bytes 98312 | tf_op jit(solution)/shard_map/ppermute | solution.py:24
  29.8 1.5 %collective-permute-start.5 = (bf16[64,256]{1,0:T(8,128)(2,1)S(1)}, bf16[64,256]{1,0:T(8,128)(2,1)S(1)}, u32[]{:S(2)}, u32[]{:S(2)}) collective-permute-start(bf16[64,256]{1,0:T(8,128)(2,1)S(1)} %get-tuple-element.15), channel_id=1, source_target_pairs={{0,4},{4,0},{8,12},{12,8},{16,20},{20,16},{24,28},{28,24},{1,5},{5... | collective-permute-start | bytes 98312 | tf_op jit(solution)/shard_map/ppermute | solution.py:24
  31.4 1.3 %collective-permute-done.7 = bf16[64,256]{1,0:T(8,128)(2,1)S(1)} collective-permute-done((bf16[64,256]{1,0:T(8,128)(2,1)S(1)}, bf16[64,256]{1,0:T(8,128)(2,1)S(1)}, u32[]{:S(2)}, u32[]{:S(2)}) %collective-permute-start.7) | collective-permute-done | bytes 32800 | tf_op jit(solution)/shard_map/ppermute | solution.py:24
  32.7 0.0 collective-permute-done.6
  32.7 1.0 %collective-permute-done.5 = bf16[64,256]{1,0:T(8,128)(2,1)S(1)} collective-permute-done((bf16[64,256]{1,0:T(8,128)(2,1)S(1)}, bf16[64,256]{1,0:T(8,128)(2,1)S(1)}, u32[]{:S(2)}, u32[]{:S(2)}) %collective-permute-start.5) | collective-permute-done | bytes 32800 | tf_op jit(solution)/shard_map/ppermute | solution.py:24
  33.8 0.1 collective-permute-start.10
  33.8 1.6 %collective-permute-start.9 = (bf16[64,256]{1,0:T(8,128)(2,1)S(1)}, bf16[64,256]{1,0:T(8,128)(2,1)S(1)}, u32[]{:S(2)}, u32[]{:S(2)}) collective-permute-start(bf16[64,256]{1,0:T(8,128)(2,1)S(1)} %add_add_fusion.1.refs_0_), channel_id=1, source_target_pairs={{0,2},{1,3},{2,0},{3,1},{4,6},{5,7},{6,4},{7,5},{8,10},{9,11},{10,... | collective-permute-start | bytes 98312 | tf_op jit(solution)/shard_map/ppermute | solution.py:24
  35.5 0.2 collective-permute-start.8
  35.7 8.4 %collective-permute-done.10.refs_3_ = bf16[64,256]{1,0:T(8,128)(2,1)S(1)} collective-permute-done((bf16[64,256]{1,0:T(8,128)(2,1)S(1)}, bf16[64,256]{1,0:T(8,128)(2,1)S(1)}, u32[]{:S(2)}, u32[]{:S(2)}) %collective-permute-start.10) | collective-permute-done | bytes 32800 | tf_op jit(solution)/shard_map/ppermute | solution.py:24
  44.1 2.1 %collective-permute-done.9.refs_2_ = bf16[64,256]{1,0:T(8,128)(2,1)S(1)} collective-permute-done((bf16[64,256]{1,0:T(8,128)(2,1)S(1)}, bf16[64,256]{1,0:T(8,128)(2,1)S(1)}, u32[]{:S(2)}, u32[]{:S(2)}) %collective-permute-start.9) | collective-permute-done | bytes 32800 | tf_op jit(solution)/shard_map/ppermute | solution.py:24
  46.2 0.0 collective-permute-done.8.refs_1_
  46.3 2.1 %cross_attention.1 = (f32[16,1024]{1,0:T(8,128)S(1)}, f32[16,1152]{1,0:T(8,128)S(1)}, f32[16,1152]{1,0:T(8,128)S(1)}, f32[16,1152]{1,0:T(8,128)S(1)}, f32[16,1152]{1,0:T(8,128)S(1)}) custom-call(bf16[64,256]{1,0:T(8,128)(2,1)S(1)} %add_add_fusion.1.refs_0_, bf16[64,256]{1,0:T(8,128)(2,1)S(1)} %collective-permute-done.8.refs_1_, ...), custom_call_target="tpu_custom_call" | custom-call | tf_op jit(solution)/shard_map/cross_attention/pallas_call | solution.py:326
  48.4 0.7 %collective-permute-start.14 = (f32[16,1152]{1,0:T(8,128)S(1)}, f32[16,1152]{1,0:T(8,128)S(1)}, u32[]{:S(2)}, u32[]{:S(2)}) collective-permute-start(f32[16,1152]{1,0:T(8,128)S(1)} %get-tuple-element.17), channel_id=1, source_target_pairs={{0,4},{4,0},{8,12},{12,8},{16,20},{20,16},{24,28},{28,24},{1,5},{5... | collective-permute-start | bytes 221192 | tf_op jit(solution)/shard_map/ppermute | solution.py:24
  49.1 1.7 %collective-permute-start.15 = (f32[16,1152]{1,0:T(8,128)S(1)}, f32[16,1152]{1,0:T(8,128)S(1)}, u32[]{:S(2)}, u32[]{:S(2)}) collective-permute-start(f32[16,1152]{1,0:T(8,128)S(1)} %get-tuple-element.18), channel_id=1, source_target_pairs={{0,8},{4,12},{8,0},{12,4},{16,24},{20,28},{24,16},{28,20},{1,9},{5... | collective-permute-start | bytes 221192 | tf_op jit(solution)/shard_map/ppermute | solution.py:24
  50.8 1.1 %collective-permute-start.16 = (f32[16,1152]{1,0:T(8,128)S(1)}, f32[16,1152]{1,0:T(8,128)S(1)}, u32[]{:S(2)}, u32[]{:S(2)}) collective-permute-start(f32[16,1152]{1,0:T(8,128)S(1)} %get-tuple-element.19), channel_id=1, source_target_pairs={{0,12},{4,8},{8,4},{12,0},{16,28},{20,24},{24,20},{28,16},{1,13},{... | collective-permute-start | bytes 221192 | tf_op jit(solution)/shard_map/ppermute | solution.py:24
  51.9 0.9 %collective-permute-done.14.refs_1_ = f32[16,1152]{1,0:T(8,128)S(1)} collective-permute-done((f32[16,1152]{1,0:T(8,128)S(1)}, f32[16,1152]{1,0:T(8,128)S(1)}, u32[]{:S(2)}, u32[]{:S(2)}) %collective-permute-start.14) | collective-permute-done | bytes 73760 | tf_op jit(solution)/shard_map/ppermute | solution.py:24
  52.8 1.1 %collective-permute-done.15.refs_2_ = f32[16,1152]{1,0:T(8,128)S(1)} collective-permute-done((f32[16,1152]{1,0:T(8,128)S(1)}, f32[16,1152]{1,0:T(8,128)S(1)}, u32[]{:S(2)}, u32[]{:S(2)}) %collective-permute-start.15) | collective-permute-done | bytes 73760 | tf_op jit(solution)/shard_map/ppermute | solution.py:24
  53.9 2.2 %collective-permute-done.16.refs_3_ = f32[16,1152]{1,0:T(8,128)S(1)} collective-permute-done((f32[16,1152]{1,0:T(8,128)S(1)}, f32[16,1152]{1,0:T(8,128)S(1)}, u32[]{:S(2)}, u32[]{:S(2)}) %collective-permute-start.16) | collective-permute-done | bytes 73760 | tf_op jit(solution)/shard_map/ppermute | solution.py:24
  56.1 0.6 merge.1.refs_0_
  56.7 0.1 collective-permute-start.19
  56.8 1.6 %collective-permute-start.18 = (f32[16,1152]{1,0:T(8,128)S(1)}, f32[16,1152]{1,0:T(8,128)S(1)}, u32[]{:S(2)}, u32[]{:S(2)}) collective-permute-start(f32[16,1152]{1,0:T(8,128)S(1)} %merge.1.refs_0_), channel_id=1, source_target_pairs={{0,2},{1,3},{2,0},{3,1},{4,6},{5,7},{6,4},{7,5},{8,10},{9,11},{10,... | collective-permute-start | bytes 221192 | tf_op jit(solution)/shard_map/ppermute | solution.py:24
  58.4 0.3 collective-permute-start.17
  58.6 2.6 %collective-permute-done.19.refs_3_ = f32[16,1152]{1,0:T(8,128)S(1)} collective-permute-done((f32[16,1152]{1,0:T(8,128)S(1)}, f32[16,1152]{1,0:T(8,128)S(1)}, u32[]{:S(2)}, u32[]{:S(2)}) %collective-permute-start.19) | collective-permute-done | bytes 73760 | tf_op jit(solution)/shard_map/ppermute | solution.py:24
  61.3 1.7 %collective-permute-done.18.refs_2_ = f32[16,1152]{1,0:T(8,128)S(1)} collective-permute-done((f32[16,1152]{1,0:T(8,128)S(1)}, f32[16,1152]{1,0:T(8,128)S(1)}, u32[]{:S(2)}, u32[]{:S(2)}) %collective-permute-start.18) | collective-permute-done | bytes 73760 | tf_op jit(solution)/shard_map/ppermute | solution.py:24
  62.9 1.7 %final.1 = bf16[16,1024]{1,0:T(8,128)(2,1)} custom-call(f32[16,1152]{1,0:T(8,128)S(1)} %merge.1.refs_0_, f32[16,1152]{1,0:T(8,128)S(1)} %collective-permute-done.17.refs_1_, f32[16,1152]{1,0:T(8,128)S(1)} %collective-permute-done.18.refs_2_, f32[16,1152]{1,0:T(8,128)S(1)} %collective-permute-done.19.refs_3_, f32[16,1024]{1,0:T(8,128)S(1)} %get-tuple-element.20.refs_4_, ...), custom_call_target="tpu_custom_call" | custom-call | tf_op jit(solution)/shard_map/final/pallas_call | solution.py:352
  (32 shorter events, 0.1 us)
Async XLA Ops:
  0.6 21.6 %collective-permute-start.11 = (bf16[256,1024]{1,0:T(8,128)(2,1)}, bf16[256,1024]{1,0:T(8,128)(2,1)S(1)}, u32[]{:S(2)}, u32[]{:S(2)}) collective-permute-start(bf16[256,1024]{1,0:T(8,128)(2,1)} %refs_4_.1), channel_id=1, source_target_pairs={{0,1},{1,0},{2,3},{3,2},{4,5},{5,4},{6,7},{7,6},{8,9},{9,8},{10,11... | collective-permute-start | bytes 1572872 | tf_op jit(solution)/shard_map/ppermute | solution.py:24
  1.2 3.3 %copy-start = (bf16[4000,1024]{1,0:T(8,128)(2,1)S(1)}, bf16[4000,1024]{1,0:T(8,128)(2,1)}, u32[]{:S(2)}) copy-start(bf16[4000,1024]{1,0:T(8,128)(2,1)} %param.17) | copy-start | bytes 24576004
  4.5 0.7 %copy-start.11 = (s32[128]{0:T(128)S(1)}, s32[128]{0:T(128)}, u32[]{:S(2)}) copy-start(s32[128]{0:T(128)} %ids_ref.1) | copy-start | bytes 1540
  5.2 15.5 %copy-start.10 = (bf16[256,1024]{1,0:T(8,128)(2,1)S(1)}, bf16[256,1024]{1,0:T(8,128)(2,1)}, u32[]{:S(2)}) copy-start(bf16[256,1024]{1,0:T(8,128)(2,1)} %refs_4_.1) | copy-start | bytes 1572868
  5.2 19.4 %copy-start.13 = (bf16[1024]{0:T(1024)(128)(2,1)S(1)}, bf16[1024]{0:T(1024)(128)(2,1)}, u32[]{:S(2)}) copy-start(bf16[1024]{0:T(1024)(128)(2,1)} %param.18) | copy-start | bytes 6148
  5.2 20.6 %copy-start.5 = (bf16[16,128,256]{2,1,0:T(8,128)(2,1)S(1)}, bf16[16,128,256]{2,1,0:T(8,128)(2,1)}, u32[]{:S(2)}) copy-start(bf16[16,128,256]{2,1,0:T(8,128)(2,1)} %pk_ref.1) | copy-start | bytes 3145732
  5.2 20.6 %copy-start.6 = (bf16[16,128,256]{2,1,0:T(8,128)(2,1)S(1)}, bf16[16,128,256]{2,1,0:T(8,128)(2,1)}, u32[]{:S(2)}) copy-start(bf16[16,128,256]{2,1,0:T(8,128)(2,1)} %pv_ref.1) | copy-start | bytes 3145732
  5.2 20.6 %copy-start.7 = (bf16[1024,256]{1,0:T(8,128)(2,1)S(1)}, bf16[1024,256]{1,0:T(8,128)(2,1)}, u32[]{:S(2)}) copy-start(bf16[1024,256]{1,0:T(8,128)(2,1)} %wq_ref.1) | copy-start | bytes 1572868
  5.2 20.6 %copy-start.8 = (bf16[1024,256]{1,0:T(8,128)(2,1)S(1)}, bf16[1024,256]{1,0:T(8,128)(2,1)}, u32[]{:S(2)}) copy-start(bf16[1024,256]{1,0:T(8,128)(2,1)} %wk_ref.1) | copy-start | bytes 1572868
  5.2 20.6 %copy-start.9 = (bf16[1024,256]{1,0:T(8,128)(2,1)S(1)}, bf16[1024,256]{1,0:T(8,128)(2,1)}, u32[]{:S(2)}) copy-start(bf16[1024,256]{1,0:T(8,128)(2,1)} %wv_ref.1) | copy-start | bytes 1572868
  5.2 20.6 %copy-start.12 = (s32[128]{0:T(128)S(1)}, s32[128]{0:T(128)}, u32[]{:S(2)}) copy-start(s32[128]{0:T(128)} %parents_ref.1) | copy-start | bytes 1540
  5.2 41.0 %copy-start.4 = (bf16[1,16,64,1024]{3,2,1,0:T(8,128)(2,1)S(1)}, bf16[1,16,64,1024]{3,2,1,0:T(8,128)(2,1)}, u32[]{:S(2)}) copy-start(bf16[1,16,64,1024]{3,2,1,0:T(8,128)(2,1)} %refs_13_.1) | copy-start | bytes 6291460
  9.2 7.8 %collective-permute-start = (bf16[32,1024]{1,0:T(8,128)(2,1)S(1)}, bf16[32,1024]{1,0:T(8,128)(2,1)S(1)}, u32[]{:S(2)}, u32[]{:S(2)}) collective-permute-start(bf16[32,1024]{1,0:T(8,128)(2,1)S(1)} %get-tuple-element.14), channel_id=1, source_target_pairs={{0,16},{4,20},{8,24},{12,28},{16,0},{20,4},{24,8},{28,12},{1,17},{... | collective-permute-start | bytes 196616 | tf_op jit(solution)/shard_map/ppermute | solution.py:24
  17.1 18.6 %copy-start.14 = (bf16[1024]{0:T(1024)(128)(2,1)S(1)}, bf16[1024]{0:T(1024)(128)(2,1)}, u32[]{:S(2)}) copy-start(bf16[1024]{0:T(1024)(128)(2,1)} %param.25) | copy-start | bytes 6148
  17.1 29.2 %copy-start.2 = (bf16[1024,1024]{1,0:T(8,128)(2,1)S(1)}, bf16[1024,1024]{1,0:T(8,128)(2,1)}, u32[]{:S(2)}) copy-start(bf16[1024,1024]{1,0:T(8,128)(2,1)} %refs_11_.1) | copy-start | bytes 6291460
  17.1 29.2 %copy-start.3 = (bf16[1,16,64,1024]{3,2,1,0:T(8,128)(2,1)S(1)}, bf16[1,16,64,1024]{3,2,1,0:T(8,128)(2,1)}, u32[]{:S(2)}) copy-start(bf16[1,16,64,1024]{3,2,1,0:T(8,128)(2,1)} %refs_12_.1) | copy-start | bytes 6291460
  17.1 5.6 %collective-permute-start.3 = (bf16[32,1024]{1,0:T(8,128)(2,1)S(1)}, bf16[32,1024]{1,0:T(8,128)(2,1)S(1)}, u32[]{:S(2)}, u32[]{:S(2)}) collective-permute-start(bf16[32,1024]{1,0:T(8,128)(2,1)S(1)} %add.21), channel_id=1, source_target_pairs={{0,12},{4,8},{8,4},{12,0},{16,28},{20,24},{24,20},{28,16},{1,13},{... | collective-permute-start | bytes 196616 | tf_op jit(solution)/shard_map/ppermute | solution.py:24
  18.8 4.5 %collective-permute-start.2 = (bf16[32,1024]{1,0:T(8,128)(2,1)S(1)}, bf16[32,1024]{1,0:T(8,128)(2,1)S(1)}, u32[]{:S(2)}, u32[]{:S(2)}) collective-permute-start(bf16[32,1024]{1,0:T(8,128)(2,1)S(1)} %add.21), channel_id=1, source_target_pairs={{0,8},{4,12},{8,0},{12,4},{16,24},{20,28},{24,16},{28,20},{1,9},{5... | collective-permute-start | bytes 196616 | tf_op jit(solution)/shard_map/ppermute | solution.py:24
  20.2 4.3 %collective-permute-start.1 = (bf16[32,1024]{1,0:T(8,128)(2,1)S(1)}, bf16[32,1024]{1,0:T(8,128)(2,1)S(1)}, u32[]{:S(2)}, u32[]{:S(2)}) collective-permute-start(bf16[32,1024]{1,0:T(8,128)(2,1)S(1)} %add.21), channel_id=1, source_target_pairs={{0,4},{4,0},{8,12},{12,8},{16,20},{20,16},{24,28},{28,24},{1,5},{5... | collective-permute-start | bytes 196616 | tf_op jit(solution)/shard_map/ppermute | solution.py:24
  20.7 25.6 %collective-permute-start.12 = (bf16[256,1024]{1,0:T(8,128)(2,1)S(1)}, bf16[256,1024]{1,0:T(8,128)(2,1)S(1)}, u32[]{:S(2)}, u32[]{:S(2)}) collective-permute-start(bf16[256,1024]{1,0:T(8,128)(2,1)S(1)} %copy-done.10), channel_id=1, source_target_pairs={{0,2},{1,3},{2,0},{3,1},{4,6},{5,7},{6,4},{7,5},{8,10},{9,11},{10,... | collective-permute-start | bytes 1572872 | tf_op jit(solution)/shard_map/ppermute | solution.py:24
  22.2 24.0 %collective-permute-start.13 = (bf16[256,1024]{1,0:T(8,128)(2,1)S(1)}, bf16[256,1024]{1,0:T(8,128)(2,1)S(1)}, u32[]{:S(2)}, u32[]{:S(2)}) collective-permute-start(bf16[256,1024]{1,0:T(8,128)(2,1)S(1)} %collective-permute-done.11.refs_5_), channel_id=1, source_target_pairs={{0,2},{1,3},{2,0},{3,1},{4,6},{5,7},{6,4},{7,5},{8,10},{9,11},{10,... | collective-permute-start | bytes 1572872 | tf_op jit(solution)/shard_map/ppermute | solution.py:24
  24.5 1.3 %collective-permute-start.4 = (bf16[32,1024]{1,0:T(8,128)(2,1)S(1)}, bf16[32,1024]{1,0:T(8,128)(2,1)S(1)}, u32[]{:S(2)}, u32[]{:S(2)}) collective-permute-start(bf16[32,1024]{1,0:T(8,128)(2,1)S(1)} %add_add_fusion.own_ref.refs_8_), channel_id=1, source_target_pairs={{0,1},{1,0},{2,3},{3,2},{4,5},{5,4},{6,7},{7,6},{8,9},{9,8},{10,11... | collective-permute-start | bytes 196616 | tf_op jit(solution)/shard_map/ppermute | solution.py:24
  27.9 4.8 %collective-permute-start.7 = (bf16[64,256]{1,0:T(8,128)(2,1)S(1)}, bf16[64,256]{1,0:T(8,128)(2,1)S(1)}, u32[]{:S(2)}, u32[]{:S(2)}) collective-permute-start(bf16[64,256]{1,0:T(8,128)(2,1)S(1)} %get-tuple-element.15), channel_id=1, source_target_pairs={{0,12},{4,8},{8,4},{12,0},{16,28},{20,24},{24,20},{28,16},{1,13},{... | collective-permute-start | bytes 98312 | tf_op jit(solution)/shard_map/ppermute | solution.py:24
  28.6 4.1 %collective-permute-start.6 = (bf16[64,256]{1,0:T(8,128)(2,1)S(1)}, bf16[64,256]{1,0:T(8,128)(2,1)S(1)}, u32[]{:S(2)}, u32[]{:S(2)}) collective-permute-start(bf16[64,256]{1,0:T(8,128)(2,1)S(1)} %get-tuple-element.15), channel_id=1, source_target_pairs={{0,8},{4,12},{8,0},{12,4},{16,24},{20,28},{24,16},{28,20},{1,9},{5... | collective-permute-start | bytes 98312 | tf_op jit(solution)/shard_map/ppermute | solution.py:24
  29.8 3.9 %collective-permute-start.5 = (bf16[64,256]{1,0:T(8,128)(2,1)S(1)}, bf16[64,256]{1,0:T(8,128)(2,1)S(1)}, u32[]{:S(2)}, u32[]{:S(2)}) collective-permute-start(bf16[64,256]{1,0:T(8,128)(2,1)S(1)} %get-tuple-element.15), channel_id=1, source_target_pairs={{0,4},{4,0},{8,12},{12,8},{16,20},{20,16},{24,28},{28,24},{1,5},{5... | collective-permute-start | bytes 98312 | tf_op jit(solution)/shard_map/ppermute | solution.py:24
  33.8 10.4 %collective-permute-start.10 = (bf16[64,256]{1,0:T(8,128)(2,1)S(1)}, bf16[64,256]{1,0:T(8,128)(2,1)S(1)}, u32[]{:S(2)}, u32[]{:S(2)}) collective-permute-start(bf16[64,256]{1,0:T(8,128)(2,1)S(1)} %add_add_fusion.1.refs_0_), channel_id=1, source_target_pairs={{0,3},{1,2},{2,1},{3,0},{4,7},{5,6},{6,5},{7,4},{8,11},{9,10},{10,... | collective-permute-start | bytes 98312 | tf_op jit(solution)/shard_map/ppermute | solution.py:24
  33.8 12.4 %collective-permute-start.9 = (bf16[64,256]{1,0:T(8,128)(2,1)S(1)}, bf16[64,256]{1,0:T(8,128)(2,1)S(1)}, u32[]{:S(2)}, u32[]{:S(2)}) collective-permute-start(bf16[64,256]{1,0:T(8,128)(2,1)S(1)} %add_add_fusion.1.refs_0_), channel_id=1, source_target_pairs={{0,2},{1,3},{2,0},{3,1},{4,6},{5,7},{6,4},{7,5},{8,10},{9,11},{10,... | collective-permute-start | bytes 98312 | tf_op jit(solution)/shard_map/ppermute | solution.py:24
  35.5 10.7 %collective-permute-start.8 = (bf16[64,256]{1,0:T(8,128)(2,1)S(1)}, bf16[64,256]{1,0:T(8,128)(2,1)S(1)}, u32[]{:S(2)}, u32[]{:S(2)}) collective-permute-start(bf16[64,256]{1,0:T(8,128)(2,1)S(1)} %add_add_fusion.1.refs_0_), channel_id=1, source_target_pairs={{0,1},{1,0},{2,3},{3,2},{4,5},{5,4},{6,7},{7,6},{8,9},{9,8},{10,11... | collective-permute-start | bytes 98312 | tf_op jit(solution)/shard_map/ppermute | solution.py:24
  35.7 27.2 %copy-start.1 = (bf16[1024,1024]{1,0:T(8,128)(2,1)S(1)}, bf16[1024,1024]{1,0:T(8,128)(2,1)}, u32[]{:S(2)}) copy-start(bf16[1024,1024]{1,0:T(8,128)(2,1)} %refs_5_.1) | copy-start | bytes 6291460
  48.4 4.4 %collective-permute-start.14 = (f32[16,1152]{1,0:T(8,128)S(1)}, f32[16,1152]{1,0:T(8,128)S(1)}, u32[]{:S(2)}, u32[]{:S(2)}) collective-permute-start(f32[16,1152]{1,0:T(8,128)S(1)} %get-tuple-element.17), channel_id=1, source_target_pairs={{0,4},{4,0},{8,12},{12,8},{16,20},{20,16},{24,28},{28,24},{1,5},{5... | collective-permute-start | bytes 221192 | tf_op jit(solution)/shard_map/ppermute | solution.py:24
  49.1 4.8 %collective-permute-start.15 = (f32[16,1152]{1,0:T(8,128)S(1)}, f32[16,1152]{1,0:T(8,128)S(1)}, u32[]{:S(2)}, u32[]{:S(2)}) collective-permute-start(f32[16,1152]{1,0:T(8,128)S(1)} %get-tuple-element.18), channel_id=1, source_target_pairs={{0,8},{4,12},{8,0},{12,4},{16,24},{20,28},{24,16},{28,20},{1,9},{5... | collective-permute-start | bytes 221192 | tf_op jit(solution)/shard_map/ppermute | solution.py:24
  50.8 5.3 %collective-permute-start.16 = (f32[16,1152]{1,0:T(8,128)S(1)}, f32[16,1152]{1,0:T(8,128)S(1)}, u32[]{:S(2)}, u32[]{:S(2)}) collective-permute-start(f32[16,1152]{1,0:T(8,128)S(1)} %get-tuple-element.19), channel_id=1, source_target_pairs={{0,12},{4,8},{8,4},{12,0},{16,28},{20,24},{24,20},{28,16},{1,13},{... | collective-permute-start | bytes 221192 | tf_op jit(solution)/shard_map/ppermute | solution.py:24
  56.7 4.6 %collective-permute-start.19 = (f32[16,1152]{1,0:T(8,128)S(1)}, f32[16,1152]{1,0:T(8,128)S(1)}, u32[]{:S(2)}, u32[]{:S(2)}) collective-permute-start(f32[16,1152]{1,0:T(8,128)S(1)} %merge.1.refs_0_), channel_id=1, source_target_pairs={{0,3},{1,2},{2,1},{3,0},{4,7},{5,6},{6,5},{7,4},{8,11},{9,10},{10,... | collective-permute-start | bytes 221192 | tf_op jit(solution)/shard_map/ppermute | solution.py:24
  56.8 6.1 %collective-permute-start.18 = (f32[16,1152]{1,0:T(8,128)S(1)}, f32[16,1152]{1,0:T(8,128)S(1)}, u32[]{:S(2)}, u32[]{:S(2)}) collective-permute-start(f32[16,1152]{1,0:T(8,128)S(1)} %merge.1.refs_0_), channel_id=1, source_target_pairs={{0,2},{1,3},{2,0},{3,1},{4,6},{5,7},{6,4},{7,5},{8,10},{9,11},{10,... | collective-permute-start | bytes 221192 | tf_op jit(solution)/shard_map/ppermute | solution.py:24
  58.4 4.6 %collective-permute-start.17 = (f32[16,1152]{1,0:T(8,128)S(1)}, f32[16,1152]{1,0:T(8,128)S(1)}, u32[]{:S(2)}, u32[]{:S(2)}) collective-permute-start(f32[16,1152]{1,0:T(8,128)S(1)} %merge.1.refs_0_), channel_id=1, source_target_pairs={{0,1},{1,0},{2,3},{3,2},{4,5},{5,4},{6,7},{7,6},{8,9},{9,8},{10,11... | collective-permute-start | bytes 221192 | tf_op jit(solution)/shard_map/ppermute | solution.py:24

commit v2 on v1

--- a/solution.py
+++ b/solution.py
@@ -8,6 +8,7 @@
 from jax.experimental.pallas import tpu as pltpu
 from jax.sharding import PartitionSpec as P
 
+
 HEADS = 16
 BEAMS = 4
 SUB = 8
@@ -52,41 +53,38 @@
     return jnp.concatenate([jnp.where(core == 0, own, other), jnp.where(core == 0, other, own)], 0)
 
 
-def gather_kernel(ids_ref, table_ref, *refs, groups, images, slab):
-    outs, (blocks, sem) = refs[:-2], refs[-2:]
+def gather_kernel(ids_ref, table_ref, *refs, slots, images, slab):
+    outs, (ids_smem, blocks, ids_sem, sem) = refs[:-4], refs[-4:]
+    pltpu.make_async_copy(ids_ref, ids_smem, ids_sem).start()
     group, _, core = place()
     first = lax.axis_index("dp") * slab
     here = images // 2
     rows = here * BEAMS
     width = blocks.shape[2]
-
-    def local_id(k):
-        slot, rest = k // rows, k % rows
-        row = ((group ^ slot) * BEAMS + rest % BEAMS) * images + core * here + rest // BEAMS
-        return ids_ref[row] - first
-
-    def start(k, carry):
-        held = jnp.clip(local_id(k), 0, slab - 1)
-        pltpu.make_async_copy(table_ref.at[held // SUB], blocks.at[k], sem).start()
-        return carry
-
-    lax.fori_loop(0, groups * rows, start, 0, unroll=SUB)
+    locals_, mine = [], []
+    pltpu.make_async_copy(ids_ref, ids_smem, ids_sem).wait()
+    for slot in slots:
+        base = (group ^ slot) * (BEAMS * images) + core * here
+        for k in range(rows):
+            local = ids_smem[base + (k % BEAMS) * images + k // BEAMS] - first
+            held = jnp.clip(local, 0, slab - 1)
+            source = table_ref.at[lax.shift_right_logical(held, int(math.log2(SUB)))]
+            pltpu.make_async_copy(source, blocks.at[len(mine)], sem).start()
+            locals_.append(held & (SUB - 1))
+            mine.append(local == held)
     pltpu.make_async_copy(blocks, blocks, sem).wait()
     sub = lax.broadcasted_iota(jnp.int32, (SUB, width), 0)
-    for slot in range(groups):
+    for out, begin in zip(outs, range(0, len(mine), rows)):
         for base in range(0, rows, 2 * SUB):
             tiles = []
             for tile in (base, base + SUB):
                 packed = jnp.zeros((SUB, width), f32)
                 for k in range(SUB):
-                    at = slot * rows + tile + k
-                    local = local_id(at)
-                    mine = jnp.logical_and(local >= 0, local < slab)
-                    place_in = jnp.clip(local, 0, slab - 1) % SUB
-                    turned = pltpu.roll(blocks[at].astype(f32), (k + SUB - place_in) % SUB, 0)
-                    packed = jnp.where(jnp.logical_and(sub == k, mine), turned, packed)
+                    at = begin + tile + k
+                    turned = pltpu.roll(blocks[at].astype(f32), (k + SUB - locals_[at]) & (SUB - 1), 0)
+                    packed = jnp.where(jnp.logical_and(sub == k, mine[at]), turned, packed)
                 tiles.append(packed)
-            outs[slot][base : base + 2 * SUB, :] = jnp.concatenate(tiles, 0).astype(bf16)
+            out[base : base + 2 * SUB, :] = jnp.concatenate(tiles, 0).astype(bf16)
 
 
 def spread(rows8, heads, head_size):
@@ -213,46 +211,76 @@
                 ]
     for k in range(BEAMS):
         theirs = pl.ds(beam ^ k, images, stride=BEAMS)
-        for part in range(width // LANES + 1):
-            messages[k][:, part * LANES : (part + 1) * LANES] = sum_scr[part, theirs, :]
-
-
-def merge(parts, head_size):
+        for part in range(width // LANES):
+            messages[k][:, part * LANES : (part + 1) * LANES] = sum_scr[part, theirs, :].astype(bf16)
+        messages[k][:, width:] = pack(sum_scr[width // LANES, theirs, :])
+
+
+def split(value, terms):
+    out = []
+    for _ in range(terms):
+        out.append(value.astype(bf16))
+        value = value - out[-1].astype(f32)
+    return out
+
+
+def pack(stats):
+    lane = lax.broadcasted_iota(jnp.int32, stats.shape, 1)
+    packed = jnp.zeros(stats.shape, f32)
+    for at, term in enumerate(split(stats, 3)):
+        term = term.astype(f32)
+        tall = pltpu.roll(term, 2 * at * HEADS, 1) if at else term
+        inside = jnp.logical_and(lane >= 2 * at * HEADS, lane < 2 * (at + 1) * HEADS)
+        packed = jnp.where(inside, tall, packed)
+    return packed.astype(bf16)
+
+
+def merge(parts, head_size, last):
+    rows = parts[0].shape[0]
     width = parts[0].shape[1] - LANES
-    lane = lax.broadcasted_iota(jnp.int32, (1, LANES), 1)
-    stats = [part[:, width:] for part in parts]
-    peak = functools.reduce(jnp.maximum, stats)
+    lane = lax.broadcasted_iota(jnp.int32, (rows, LANES), 1)
+    peaks, totals = [], []
+    for part in parts:
+        stat = part[:, width:].astype(f32)
+        stat = stat + pltpu.roll(stat, LANES - 2 * HEADS, 1) + pltpu.roll(stat, LANES - 4 * HEADS, 1)
+        peaks.append(stat)
+        totals.append(pltpu.roll(stat, LANES - HEADS, 1))
+    peak = functools.reduce(jnp.maximum, peaks)
+    scales = [jnp.where(lane < HEADS, jnp.exp(p - peak), 0.0) for p in peaks]
+    total = sum(scale * t for scale, t in zip(scales, totals))
+    if last:
+        total = jnp.where(lane < HEADS, total, 1.0)
+        scales = [scale / total for scale in scales]
     row = lax.broadcasted_iota(jnp.int32, (LANES, width), 0)
     owner = lax.broadcasted_iota(jnp.int32, (LANES, width), 1) // head_size
-    widen = (row == owner).astype(f32)
-    total = 0.0
+    widen = (row == owner).astype(bf16)
+    high, low = split(jnp.concatenate(scales, 0), 2)
+    wide = dot(jnp.concatenate([high, low], 0), widen)
+    many = len(parts) * rows
+    wide = wide[:many] + wide[many:]
     sums = 0.0
-    for part, stat in zip(parts, stats):
-        scale = jnp.where(lane < HEADS, jnp.exp(stat - peak), 0.0)
-        total = total + pltpu.roll(stat, LANES - HEADS, 1) * scale
-        sums = sums + part[:, :width] * jnp.dot(scale, widen, precision=lax.Precision.HIGHEST)
-    return sums, peak, total, lane, widen
+    for k, part in enumerate(parts):
+        sums = sums + part[:, :width].astype(f32) * wide[k * rows : (k + 1) * rows]
+    stats = jnp.where(lane < HEADS, peak, pltpu.roll(total, HEADS, 1))
+    return sums, jnp.where(lane < 2 * HEADS, stats, 0.0)
 
 
 def merge_kernel(*refs, head_size):
     parts, out_ref = [ref[...] for ref in refs[:-1]], refs[-1]
-    sums, peak, total, lane, _ = merge(parts, head_size)
+    sums, stats = merge(parts, head_size, False)
     width = sums.shape[1]
-    out_ref[:, :width] = sums
-    out_ref[:, width:] = jnp.where(lane < HEADS, peak, pltpu.roll(total, HEADS, 1))
+    out_ref[:, :width] = sums.astype(bf16)
+    out_ref[:, width:] = pack(stats)
 
 
 def final_kernel(*refs, head_size):
     parts = [ref[...] for ref in refs[:-3]]
     middle_ref, weight_ref, out_ref = refs[-3:]
-    sums, _, total, lane, widen = merge(parts, head_size)
-    total = jnp.where(lane < HEADS, total, 1.0)
-    wide = jnp.dot(total, widen, precision=lax.Precision.HIGHEST)
-    context = (sums / wide).astype(bf16)
-    out_ref[...] = (middle_ref[...] + dot(context, weight_ref[...])).astype(bf16)
-
-
-def shards(
+    context, _ = merge(parts, head_size, True)
+    out_ref[...] = (middle_ref[...] + dot(context.astype(bf16), weight_ref[...])).astype(bf16)
+
+
+def step(
     token_ids,
     parents,
     embedding,
@@ -269,7 +297,7 @@
     image_keys,
     image_values,
 ):
-    images, length, width_here = past_keys.shape
+    images, _, width_here = past_keys.shape
     slab, width = embedding.shape
     head_size = width // HEADS
     groups = lax.axis_size("dp") // BEAMS
@@ -279,30 +307,45 @@
     smem = pl.BlockSpec(memory_space=pltpu.SMEM)
     vmem = pl.BlockSpec(memory_space=pltpu.VMEM)
 
-    outputs = [output_weight]
-    mask = 1
-    while mask < patches:
-        outputs = outputs + [swap(piece, "patch", mask) for piece in outputs]
-        mask *= 2
-
-    slots = pl.pallas_call(
-        functools.partial(gather_kernel, groups=groups, images=images, slab=slab),
-        out_shape=[jax.ShapeDtypeStruct((half, width), bf16)] * groups,
-        in_specs=[smem, pl.BlockSpec(memory_space=pl.ANY)],
-        out_specs=[vmem] * groups,
-        scratch_shapes=[
-            pltpu.VMEM((groups * half, SUB, width), bf16),
-            pltpu.SemaphoreType.DMA,
-        ],
-        compiler_params=params(16),
-        name="gather",
-    )(token_ids, embedding.reshape(slab // SUB, SUB, width))
+    weights = {0: output_weight}
+    mask = patches // 2
+    while mask > 1:
+        weights |= {k ^ mask: swap(piece, "patch", mask) for k, piece in weights.items()}
+        mask //= 2
+
+    table = embedding.reshape(slab // SUB, SUB, width)
+    table = pltpu.with_memory_space_constraint(table, pltpu.HBM)
+    ids = pltpu.with_memory_space_constraint(token_ids, pltpu.HBM)
+
+    def gather(slots):
+        return pl.pallas_call(
+            functools.partial(gather_kernel, slots=slots, images=images, slab=slab),
+            out_shape=[jax.ShapeDtypeStruct((half, width), bf16)] * len(slots),
+            in_specs=[pl.BlockSpec(memory_space=pltpu.HBM)] * 2,
+            out_specs=[vmem] * len(slots),
+            scratch_shapes=[
+                pltpu.SMEM(token_ids.shape, jnp.int32),
+                pltpu.VMEM((len(slots) * half, SUB, width), bf16),
+                pltpu.SemaphoreType.DMA,
+                pltpu.SemaphoreType.DMA,
+            ],
+            compiler_params=params(8),
+        )(ids, table)
+
+    if groups > 1:
+        keep = groups // 2
+        sent = [swap(b, "dp", keep * BEAMS) for b in gather(range(keep, groups))]
+        slots = [a + b for a, b in zip(gather(range(keep)), sent)]
+    else:
+        slots = gather(range(groups))
     while len(slots) > 1:
         keep = len(slots) // 2
         slots = [a + swap(b, "dp", keep * BEAMS) for a, b in zip(slots[:keep], slots[keep:])]
     own = slots[0]
-    own = own + swap(own, "dp", 1) + swap(own, "dp", 2) + swap(own, "dp", 3)
+    own = own + sum(swap(own, "dp", k) for k in range(1, BEAMS))
     other = swap(own, "patch", 1)
+    weights |= {k ^ 1: swap(piece, "patch", 1) for k, piece in weights.items()}
+    outputs = [weights[k] for k in range(patches)]
 
     context, new_key, new_value = pl.pallas_call(
         functools.partial(self_kernel, head_size=head_size),
@@ -318,7 +361,7 @@
         name="self_attention",
     )(parents, own, other, self_gain.reshape(1, width), query_weight, key_weight, value_weight,
       past_keys, past_values)
-    context = context + swap(context, "dp", 1) + swap(context, "dp", 2) + swap(context, "dp", 3)
+    context = context + sum(swap(context, "dp", k) for k in range(1, BEAMS))
     contexts = [context] + [swap(context, "patch", k) for k in range(1, patches)]
 
     patch_count = image_keys.shape[2]
@@ -326,7 +369,7 @@
     middle, *messages = pl.pallas_call(
         functools.partial(cross_kernel, pieces=patches, head_size=head_size),
         out_shape=[jax.ShapeDtypeStruct((images, width), f32)]
-        + [jax.ShapeDtypeStruct((images, width + LANES), f32)] * BEAMS,
+        + [jax.ShapeDtypeStruct((images, width + LANES), bf16)] * BEAMS,
         in_specs=[vmem] * (2 * patches + 6),
         out_specs=[vmem] * (1 + BEAMS),
         scratch_shapes=[
@@ -339,10 +382,10 @@
         name="cross_attention",
     )(*contexts, *outputs, own, other, cross_gain.reshape(1, width), cross_query, image_keys,
       image_values)
-    parts = [messages[0]] + [swap(messages[k], "dp", k) for k in range(1, BEAMS)]
+    parts = [swap(messages[k], "dp", k) for k in range(BEAMS - 1, 0, -1)] + [messages[0]]
     part = pl.pallas_call(
         functools.partial(merge_kernel, head_size=head_size),
-        out_shape=jax.ShapeDtypeStruct((images, width + LANES), f32),
+        out_shape=jax.ShapeDtypeStruct((images, width + LANES), bf16),
         in_specs=[vmem] * BEAMS,
         out_specs=vmem,
         compiler_params=params(8),
@@ -379,4 +422,4 @@
         P("dp", None, "patch", None),
     )
     out_specs = (P("dp", None), P("dp", "patch"), P("dp", "patch"))
-    return jax.shard_map(shards, mesh=mesh, in_specs=in_specs, out_specs=out_specs, check_vma=False)
+    return jax.shard_map(step, mesh=mesh, in_specs=in_specs, out_specs=out_specs, check_vma=False)

time: 64.8 us -> 48.1 us (0.74)
  waiting for transfers between devices: 28.4 us -> 15.5 us
  local copies, waits for them, and re-layouts: 4.05 us -> 0.09 us
    ppermute x20, waiting for transfers between devices: 28.4 us -> 15.5 us  [swap(): return lax.ppermute(value, axis, pairs)]
    unnamed x30 -> x26, local copies, waits for them, and re-layouts: 4.04 us -> 0.08 us
    pallas_call x5 -> x6, Pallas kernels: 10.5 us -> 11 us  [the longest x2 5.16 us: gather(): pl.pallas_call(functools.partial(gather_kernel, slots=slots, images=image...]
  transfers between devices with their start and end apart: 20 -> 20, of which waited for: 13 -> 16; matrix products, arithmetic and copies ran while one was open for 0% -> 0% of each run, Pallas kernels for 9% -> 15%
where the time goes in v2:
time: 48.1 us; the launch traced here: 47.7 us
  starting transfers between devices  20.1 us (42%)
  waiting for transfers between devices  15.5 us (32%)
  Pallas kernels  11 us (23%)
  between operations  0.87 us (2%)
    ppermute x20, starting transfers between devices, swap(): return lax.ppermute(value, axis, pairs)  20.1 us
    ppermute x20, waiting for transfers between devices, swap(): return lax.ppermute(value, axis, pairs)  15.5 us
    pallas_call x2, Pallas kernels, gather(): pl.pallas_call(functools.partial(gather_kernel, slots=slots, images=image...  5.16 us
    pallas_call x1, Pallas kernels, step(): pl.pallas_call(functools.partial(cross_kernel, pieces=patches, head_size=...  2.2 us
    pallas_call x1, Pallas kernels, step(): pl.pallas_call(functools.partial(self_kernel, head_size=head_size), out_s...  2.06 us
    pallas_call x1, Pallas kernels, step(): pl.pallas_call(functools.partial(final_kernel, head_size=head_size), out_...  1.29 us
  transfers between devices with their start and end apart: 20, of which 16 were waited for; matrix products, arithmetic and copies ran while one was open for 0% of the time, Pallas kernels for 15%

profile of v2, /device:TPU:0, one launch (start us, length us, event | category | flops | bytes accessed | tf_op | source)
XLA Modules:
  0.0 47.7 jit_solution(11246233910614479232)
XLA Ops:
  0.6 3.1 %collective-permute-start.12 = (bf16[256,1024]{1,0:T(8,128)(2,1)}, bf16[256,1024]{1,0:T(8,128)(2,1)S(1)}, u32[]{:S(2)}, u32[]{:S(2)}) collective-permute-start(bf16[256,1024]{1,0:T(8,128)(2,1)} %refs_4_.1), channel_id=1, source_target_pairs={{0,2},{1,3},{2,0},{3,1},{4,6},{5,7},{6,4},{7,5},{8,10},{9,11},{10,... | collective-permute-start | bytes 1572872 | tf_op jit(solution)/shard_map/ppermute | solution.py:25
  3.7 2.5 %shard_map.167 = bf16[32,1024]{1,0:T(8,128)(2,1)S(1)} custom-call(s32[128]{0:T(128)} %ids_ref.3, bf16[500,8,1024]{2,1,0:T(8,128)(2,1)} %bitcast.1), custom_call_target="tpu_custom_call" | custom-call | tf_op jit(solution)/shard_map/pallas_call | solution.py:321
  6.2 0.0 copy-start.9
  6.2 0.0 copy-start.11
  6.3 0.0 copy-start.5
  6.3 0.0 copy-start.6
  6.3 0.0 copy-start.10
  6.3 2.6 %collective-permute-start = (bf16[32,1024]{1,0:T(8,128)(2,1)S(1)}, bf16[32,1024]{1,0:T(8,128)(2,1)S(1)}, u32[]{:S(2)}, u32[]{:S(2)}) collective-permute-start(bf16[32,1024]{1,0:T(8,128)(2,1)S(1)} %shard_map.167), channel_id=1, source_target_pairs={{0,16},{4,20},{8,24},{12,28},{16,0},{20,4},{24,8},{28,12},{1,17},{... | collective-permute-start | bytes 196616 | tf_op jit(solution)/shard_map/ppermute | solution.py:25
  8.9 2.6 %shard_map.166 = bf16[32,1024]{1,0:T(8,128)(2,1)S(1)} custom-call(s32[128]{0:T(128)} %ids_ref.3, bf16[500,8,1024]{2,1,0:T(8,128)(2,1)} %bitcast.2), custom_call_target="tpu_custom_call" | custom-call | tf_op jit(solution)/shard_map/pallas_call | solution.py:321
  11.5 0.2 collective-permute-done
  11.7 0.0 copy-start.12
  11.7 0.0 copy-start.1
  11.8 2.5 %collective-permute-start.3 = (bf16[32,1024]{1,0:T(8,128)(2,1)S(1)}, bf16[32,1024]{1,0:T(8,128)(2,1)S(1)}, u32[]{:S(2)}, u32[]{:S(2)}) collective-permute-start(bf16[32,1024]{1,0:T(8,128)(2,1)S(1)} %add.21), channel_id=1, source_target_pairs={{0,12},{4,8},{8,4},{12,0},{16,28},{20,24},{24,20},{28,16},{1,13},{... | collective-permute-start | bytes 196616 | tf_op jit(solution)/shard_map/ppermute | solution.py:25
  14.2 0.6 %collective-permute-start.2 = (bf16[32,1024]{1,0:T(8,128)(2,1)S(1)}, bf16[32,1024]{1,0:T(8,128)(2,1)S(1)}, u32[]{:S(2)}, u32[]{:S(2)}) collective-permute-start(bf16[32,1024]{1,0:T(8,128)(2,1)S(1)} %add.21), channel_id=1, source_target_pairs={{0,8},{4,12},{8,0},{12,4},{16,24},{20,28},{24,16},{28,20},{1,9},{5... | collective-permute-start | bytes 196616 | tf_op jit(solution)/shard_map/ppermute | solution.py:25
  14.9 0.4 collective-permute-start.1
  15.3 0.5 %collective-permute-done.12.refs_6_ = bf16[256,1024]{1,0:T(8,128)(2,1)S(1)} collective-permute-done((bf16[256,1024]{1,0:T(8,128)(2,1)}, bf16[256,1024]{1,0:T(8,128)(2,1)S(1)}, u32[]{:S(2)}, u32[]{:S(2)}) %collective-permute-start.12) | collective-permute-done | bytes 524320 | tf_op jit(solution)/shard_map/ppermute | solution.py:25
  15.8 0.0 collective-permute-start.13
  15.8 1.4 %collective-permute-done.3 = bf16[32,1024]{1,0:T(8,128)(2,1)S(1)} collective-permute-done((bf16[32,1024]{1,0:T(8,128)(2,1)S(1)}, bf16[32,1024]{1,0:T(8,128)(2,1)S(1)}, u32[]{:S(2)}, u32[]{:S(2)}) %collective-permute-start.3) | collective-permute-done | bytes 65568 | tf_op jit(solution)/shard_map/ppermute | solution.py:25
  17.2 1.3 %collective-permute-done.2 = bf16[32,1024]{1,0:T(8,128)(2,1)S(1)} collective-permute-done((bf16[32,1024]{1,0:T(8,128)(2,1)S(1)}, bf16[32,1024]{1,0:T(8,128)(2,1)S(1)}, u32[]{:S(2)}, u32[]{:S(2)}) %collective-permute-start.2) | collective-permute-done | bytes 65568 | tf_op jit(solution)/shard_map/ppermute | solution.py:25
  18.5 0.6 %collective-permute-done.1 = bf16[32,1024]{1,0:T(8,128)(2,1)S(1)} collective-permute-done((bf16[32,1024]{1,0:T(8,128)(2,1)S(1)}, bf16[32,1024]{1,0:T(8,128)(2,1)S(1)}, u32[]{:S(2)}, u32[]{:S(2)}) %collective-permute-start.1) | collective-permute-done | bytes 65568 | tf_op jit(solution)/shard_map/ppermute | solution.py:25
  19.2 0.1 collective-permute-start.4
  19.3 1.2 %collective-permute-done.4.other_ref.refs_9_ = bf16[32,1024]{1,0:T(8,128)(2,1)S(1)} collective-permute-done((bf16[32,1024]{1,0:T(8,128)(2,1)S(1)}, bf16[32,1024]{1,0:T(8,128)(2,1)S(1)}, u32[]{:S(2)}, u32[]{:S(2)}) %collective-permute-start.4) | collective-permute-done | bytes 65568 | tf_op jit(solution)/shard_map/ppermute | solution.py:25
  20.5 2.1 %self_attention.1 = (bf16[64,256]{1,0:T(8,128)(2,1)S(1)}, bf16[16,256]{1,0:T(8,128)(2,1)}, bf16[16,256]{1,0:T(8,128)(2,1)}) custom-call(s32[128]{0:T(128)S(1)} %copy-done.10, bf16[32,1024]{1,0:T(8,128)(2,1)S(1)} %add_add_fusion.own_ref.refs_8_, bf16[32,1024]{1,0:T(8,128)(2,1)S(1)} %collective-permute-done.4.other_ref.refs_9_, ...), custom_call_target="tpu_custom_call" | custom-call | tf_op jit(solution)/shard_map/self_attention/pallas_call | solution.py:350
  22.6 1.4 %collective-permute-start.7 = (bf16[64,256]{1,0:T(8,128)(2,1)S(1)}, bf16[64,256]{1,0:T(8,128)(2,1)S(1)}, u32[]{:S(2)}, u32[]{:S(2)}) collective-permute-start(bf16[64,256]{1,0:T(8,128)(2,1)S(1)} %get-tuple-element.11), channel_id=1, source_target_pairs={{0,12},{4,8},{8,4},{12,0},{16,28},{20,24},{24,20},{28,16},{1,13},{... | collective-permute-start | bytes 98312 | tf_op jit(solution)/shard_map/ppermute | solution.py:25
  23.9 0.6 %collective-permute-start.6 = (bf16[64,256]{1,0:T(8,128)(2,1)S(1)}, bf16[64,256]{1,0:T(8,128)(2,1)S(1)}, u32[]{:S(2)}, u32[]{:S(2)}) collective-permute-start(bf16[64,256]{1,0:T(8,128)(2,1)S(1)} %get-tuple-element.11), channel_id=1, source_target_pairs={{0,8},{4,12},{8,0},{12,4},{16,24},{20,28},{24,16},{28,20},{1,9},{5... | collective-permute-start | bytes 98312 | tf_op jit(solution)/shard_map/ppermute | solution.py:25
  24.5 1.6 %collective-permute-start.5 = (bf16[64,256]{1,0:T(8,128)(2,1)S(1)}, bf16[64,256]{1,0:T(8,128)(2,1)S(1)}, u32[]{:S(2)}, u32[]{:S(2)}) collective-permute-start(bf16[64,256]{1,0:T(8,128)(2,1)S(1)} %get-tuple-element.11), channel_id=1, source_target_pairs={{0,4},{4,0},{8,12},{12,8},{16,20},{20,16},{24,28},{28,24},{1,5},{5... | collective-permute-start | bytes 98312 | tf_op jit(solution)/shard_map/ppermute | solution.py:25
  26.1 1.4 %collective-permute-done.7 = bf16[64,256]{1,0:T(8,128)(2,1)S(1)} collective-permute-done((bf16[64,256]{1,0:T(8,128)(2,1)S(1)}, bf16[64,256]{1,0:T(8,128)(2,1)S(1)}, u32[]{:S(2)}, u32[]{:S(2)}) %collective-permute-start.7) | collective-permute-done | bytes 32800 | tf_op jit(solution)/shard_map/ppermute | solution.py:25
  27.4 0.4 collective-permute-done.6
  27.9 0.6 %collective-permute-done.5 = bf16[64,256]{1,0:T(8,128)(2,1)S(1)} collective-permute-done((bf16[64,256]{1,0:T(8,128)(2,1)S(1)}, bf16[64,256]{1,0:T(8,128)(2,1)S(1)}, u32[]{:S(2)}, u32[]{:S(2)}) %collective-permute-start.5) | collective-permute-done | bytes 32800 | tf_op jit(solution)/shard_map/ppermute | solution.py:25
  28.4 0.1 collective-permute-start.10
  28.5 0.6 %collective-permute-start.9 = (bf16[64,256]{1,0:T(8,128)(2,1)S(1)}, bf16[64,256]{1,0:T(8,128)(2,1)S(1)}, u32[]{:S(2)}, u32[]{:S(2)}) collective-permute-start(bf16[64,256]{1,0:T(8,128)(2,1)S(1)} %add_add_fusion.1.refs_0_), channel_id=1, source_target_pairs={{0,2},{1,3},{2,0},{3,1},{4,6},{5,7},{6,4},{7,5},{8,10},{9,11},{10,... | collective-permute-start | bytes 98312 | tf_op jit(solution)/shard_map/ppermute | solution.py:25
  29.1 1.3 %collective-permute-start.8 = (bf16[64,256]{1,0:T(8,128)(2,1)S(1)}, bf16[64,256]{1,0:T(8,128)(2,1)S(1)}, u32[]{:S(2)}, u32[]{:S(2)}) collective-permute-start(bf16[64,256]{1,0:T(8,128)(2,1)S(1)} %add_add_fusion.1.refs_0_), channel_id=1, source_target_pairs={{0,1},{1,0},{2,3},{3,2},{4,5},{5,4},{6,7},{7,6},{8,9},{9,8},{10,11... | collective-permute-start | bytes 98312 | tf_op jit(solution)/shard_map/ppermute | solution.py:25
  30.4 1.5 %collective-permute-done.10.refs_3_ = bf16[64,256]{1,0:T(8,128)(2,1)S(1)} collective-permute-done((bf16[64,256]{1,0:T(8,128)(2,1)S(1)}, bf16[64,256]{1,0:T(8,128)(2,1)S(1)}, u32[]{:S(2)}, u32[]{:S(2)}) %collective-permute-start.10) | collective-permute-done | bytes 32800 | tf_op jit(solution)/shard_map/ppermute | solution.py:25
  31.8 0.7 %collective-permute-done.9.refs_2_ = bf16[64,256]{1,0:T(8,128)(2,1)S(1)} collective-permute-done((bf16[64,256]{1,0:T(8,128)(2,1)S(1)}, bf16[64,256]{1,0:T(8,128)(2,1)S(1)}, u32[]{:S(2)}, u32[]{:S(2)}) %collective-permute-start.9) | collective-permute-done | bytes 32800 | tf_op jit(solution)/shard_map/ppermute | solution.py:25
  32.6 2.2 %cross_attention.1 = (f32[16,1024]{1,0:T(8,128)S(1)}, bf16[16,1152]{1,0:T(8,128)(2,1)S(1)}, bf16[16,1152]{1,0:T(8,128)(2,1)S(1)}, bf16[16,1152]{1,0:T(8,128)(2,1)S(1)}, bf16[16,1152]{1,0:T(8,128)(2,1)S(1)}) custom-call(bf16[64,256]{1,0:T(8,128)(2,1)S(1)} %add_add_fusion.1.refs_0_, bf16[64,256]{1,0:T(8,128)(2,1)S(1)} %collective-permute-done.8.refs_1_, ...), custom_call_target="tpu_custom_call" | custom-call | tf_op jit(solution)/shard_map/cross_attention/pallas_call | solution.py:369
  34.8 2.5 %collective-permute-start.14 = (bf16[16,1152]{1,0:T(8,128)(2,1)S(1)}, bf16[16,1152]{1,0:T(8,128)(2,1)S(1)}, u32[]{:S(2)}, u32[]{:S(2)}) collective-permute-start(bf16[16,1152]{1,0:T(8,128)(2,1)S(1)} %get-tuple-element.12), channel_id=1, source_target_pairs={{0,12},{4,8},{8,4},{12,0},{16,28},{20,24},{24,20},{28,16},{1,13},{... | collective-permute-start | bytes 110600 | tf_op jit(solution)/shard_map/ppermute | solution.py:25
  37.2 0.6 %collective-permute-start.15 = (bf16[16,1152]{1,0:T(8,128)(2,1)S(1)}, bf16[16,1152]{1,0:T(8,128)(2,1)S(1)}, u32[]{:S(2)}, u32[]{:S(2)}) collective-permute-start(bf16[16,1152]{1,0:T(8,128)(2,1)S(1)} %get-tuple-element.13), channel_id=1, source_target_pairs={{0,8},{4,12},{8,0},{12,4},{16,24},{20,28},{24,16},{28,20},{1,9},{5... | collective-permute-start | bytes 110600 | tf_op jit(solution)/shard_map/ppermute | solution.py:25
  37.9 0.5 collective-permute-start.16
  38.3 1.7 %collective-permute-done.14.refs_0_ = bf16[16,1152]{1,0:T(8,128)(2,1)S(1)} collective-permute-done((bf16[16,1152]{1,0:T(8,128)(2,1)S(1)}, bf16[16,1152]{1,0:T(8,128)(2,1)S(1)}, u32[]{:S(2)}, u32[]{:S(2)}) %collective-permute-start.14) | collective-permute-done | bytes 36896 | tf_op jit(solution)/shard_map/ppermute | solution.py:25
  40.1 1.1 %collective-permute-done.15.refs_1_ = bf16[16,1152]{1,0:T(8,128)(2,1)S(1)} collective-permute-done((bf16[16,1152]{1,0:T(8,128)(2,1)S(1)}, bf16[16,1152]{1,0:T(8,128)(2,1)S(1)}, u32[]{:S(2)}, u32[]{:S(2)}) %collective-permute-start.15) | collective-permute-done | bytes 36896 | tf_op jit(solution)/shard_map/ppermute | solution.py:25
  41.2 0.6 %collective-permute-done.16.refs_2_ = bf16[16,1152]{1,0:T(8,128)(2,1)S(1)} collective-permute-done((bf16[16,1152]{1,0:T(8,128)(2,1)S(1)}, bf16[16,1152]{1,0:T(8,128)(2,1)S(1)}, u32[]{:S(2)}, u32[]{:S(2)}) %collective-permute-start.16) | collective-permute-done | bytes 36896 | tf_op jit(solution)/shard_map/ppermute | solution.py:25
  41.8 0.3 merge.1.refs_0_
  42.2 0.1 collective-permute-start.19
  42.2 0.6 %collective-permute-start.18 = (bf16[16,1152]{1,0:T(8,128)(2,1)S(1)}, bf16[16,1152]{1,0:T(8,128)(2,1)S(1)}, u32[]{:S(2)}, u32[]{:S(2)}) collective-permute-start(bf16[16,1152]{1,0:T(8,128)(2,1)S(1)} %merge.1.refs_0_), channel_id=1, source_target_pairs={{0,2},{1,3},{2,0},{3,1},{4,6},{5,7},{6,4},{7,5},{8,10},{9,11},{10,... | collective-permute-start | bytes 110600 | tf_op jit(solution)/shard_map/ppermute | solution.py:25
  42.8 1.3 %collective-permute-start.17 = (bf16[16,1152]{1,0:T(8,128)(2,1)S(1)}, bf16[16,1152]{1,0:T(8,128)(2,1)S(1)}, u32[]{:S(2)}, u32[]{:S(2)}) collective-permute-start(bf16[16,1152]{1,0:T(8,128)(2,1)S(1)} %merge.1.refs_0_), channel_id=1, source_target_pairs={{0,1},{1,0},{2,3},{3,2},{4,5},{5,4},{6,7},{7,6},{8,9},{9,8},{10,11... | collective-permute-start | bytes 110600 | tf_op jit(solution)/shard_map/ppermute | solution.py:25
  44.1 1.5 %collective-permute-done.19.refs_3_ = bf16[16,1152]{1,0:T(8,128)(2,1)S(1)} collective-permute-done((bf16[16,1152]{1,0:T(8,128)(2,1)S(1)}, bf16[16,1152]{1,0:T(8,128)(2,1)S(1)}, u32[]{:S(2)}, u32[]{:S(2)}) %collective-permute-start.19) | collective-permute-done | bytes 36896 | tf_op jit(solution)/shard_map/ppermute | solution.py:25
  45.6 0.8 %collective-permute-done.18.refs_2_ = bf16[16,1152]{1,0:T(8,128)(2,1)S(1)} collective-permute-done((bf16[16,1152]{1,0:T(8,128)(2,1)S(1)}, bf16[16,1152]{1,0:T(8,128)(2,1)S(1)}, u32[]{:S(2)}, u32[]{:S(2)}) %collective-permute-start.18) | collective-permute-done | bytes 36896 | tf_op jit(solution)/shard_map/ppermute | solution.py:25
  46.4 1.3 %final.1 = bf16[16,1024]{1,0:T(8,128)(2,1)} custom-call(bf16[16,1152]{1,0:T(8,128)(2,1)S(1)} %merge.1.refs_0_, bf16[16,1152]{1,0:T(8,128)(2,1)S(1)} %collective-permute-done.17.refs_1_, bf16[16,1152]{1,0:T(8,128)(2,1)S(1)} %collective-permute-done.18.refs_2_, bf16[16,1152]{1,0:T(8,128)(2,1)S(1)} %collective-permute-done.19.refs_3_, ...), custom_call_target="tpu_custom_call" | custom-call | tf_op jit(solution)/shard_map/final/pallas_call | solution.py:395
  (29 shorter events, 0.1 us)
Async XLA Ops:
  0.6 15.2 %collective-permute-start.12 = (bf16[256,1024]{1,0:T(8,128)(2,1)}, bf16[256,1024]{1,0:T(8,128)(2,1)S(1)}, u32[]{:S(2)}, u32[]{:S(2)}) collective-permute-start(bf16[256,1024]{1,0:T(8,128)(2,1)} %refs_4_.1), channel_id=1, source_target_pairs={{0,2},{1,3},{2,0},{3,1},{4,6},{5,7},{6,4},{7,5},{8,10},{9,11},{10,... | collective-permute-start | bytes 1572872 | tf_op jit(solution)/shard_map/ppermute | solution.py:25
  6.2 9.1 %copy-start.9 = (bf16[256,1024]{1,0:T(8,128)(2,1)S(1)}, bf16[256,1024]{1,0:T(8,128)(2,1)}, u32[]{:S(2)}) copy-start(bf16[256,1024]{1,0:T(8,128)(2,1)} %refs_4_.1) | copy-start | bytes 1572868
  6.2 13.0 %copy-start.11 = (bf16[1024]{0:T(1024)(128)(2,1)S(1)}, bf16[1024]{0:T(1024)(128)(2,1)}, u32[]{:S(2)}) copy-start(bf16[1024]{0:T(1024)(128)(2,1)} %param.18) | copy-start | bytes 6148
  6.3 14.2 %copy-start.4 = (bf16[16,128,256]{2,1,0:T(8,128)(2,1)S(1)}, bf16[16,128,256]{2,1,0:T(8,128)(2,1)}, u32[]{:S(2)}) copy-start(bf16[16,128,256]{2,1,0:T(8,128)(2,1)} %pk_ref.1) | copy-start | bytes 3145732
  6.3 14.2 %copy-start.5 = (bf16[16,128,256]{2,1,0:T(8,128)(2,1)S(1)}, bf16[16,128,256]{2,1,0:T(8,128)(2,1)}, u32[]{:S(2)}) copy-start(bf16[16,128,256]{2,1,0:T(8,128)(2,1)} %pv_ref.1) | copy-start | bytes 3145732
  6.3 14.2 %copy-start.6 = (bf16[1024,256]{1,0:T(8,128)(2,1)S(1)}, bf16[1024,256]{1,0:T(8,128)(2,1)}, u32[]{:S(2)}) copy-start(bf16[1024,256]{1,0:T(8,128)(2,1)} %wq_ref.1) | copy-start | bytes 1572868
  6.3 14.2 %copy-start.7 = (bf16[1024,256]{1,0:T(8,128)(2,1)S(1)}, bf16[1024,256]{1,0:T(8,128)(2,1)}, u32[]{:S(2)}) copy-start(bf16[1024,256]{1,0:T(8,128)(2,1)} %wk_ref.1) | copy-start | bytes 1572868
  6.3 14.2 %copy-start.8 = (bf16[1024,256]{1,0:T(8,128)(2,1)S(1)}, bf16[1024,256]{1,0:T(8,128)(2,1)}, u32[]{:S(2)}) copy-start(bf16[1024,256]{1,0:T(8,128)(2,1)} %wv_ref.1) | copy-start | bytes 1572868
  6.3 14.2 %copy-start.10 = (s32[128]{0:T(128)S(1)}, s32[128]{0:T(128)}, u32[]{:S(2)}) copy-start(s32[128]{0:T(128)} %parents_ref.1) | copy-start | bytes 1540
  6.3 5.4 %collective-permute-start = (bf16[32,1024]{1,0:T(8,128)(2,1)S(1)}, bf16[32,1024]{1,0:T(8,128)(2,1)S(1)}, u32[]{:S(2)}, u32[]{:S(2)}) collective-permute-start(bf16[32,1024]{1,0:T(8,128)(2,1)S(1)} %shard_map.167), channel_id=1, source_target_pairs={{0,16},{4,20},{8,24},{12,28},{16,0},{20,4},{24,8},{28,12},{1,17},{... | collective-permute-start | bytes 196616 | tf_op jit(solution)/shard_map/ppermute | solution.py:25
  8.9 23.7 %copy-start.3 = (bf16[1,16,64,1024]{3,2,1,0:T(8,128)(2,1)S(1)}, bf16[1,16,64,1024]{3,2,1,0:T(8,128)(2,1)}, u32[]{:S(2)}) copy-start(bf16[1,16,64,1024]{3,2,1,0:T(8,128)(2,1)} %refs_13_.1) | copy-start | bytes 6291460
  11.7 18.6 %copy-start.12 = (bf16[1024]{0:T(1024)(128)(2,1)S(1)}, bf16[1024]{0:T(1024)(128)(2,1)}, u32[]{:S(2)}) copy-start(bf16[1024]{0:T(1024)(128)(2,1)} %param.25) | copy-start | bytes 6148
  11.7 20.8 %copy-start.1 = (bf16[1024,1024]{1,0:T(8,128)(2,1)S(1)}, bf16[1024,1024]{1,0:T(8,128)(2,1)}, u32[]{:S(2)}) copy-start(bf16[1024,1024]{1,0:T(8,128)(2,1)} %refs_11_.1) | copy-start | bytes 6291460
  11.7 20.8 %copy-start.2 = (bf16[1,16,64,1024]{3,2,1,0:T(8,128)(2,1)S(1)}, bf16[1,16,64,1024]{3,2,1,0:T(8,128)(2,1)}, u32[]{:S(2)}) copy-start(bf16[1,16,64,1024]{3,2,1,0:T(8,128)(2,1)} %refs_12_.1) | copy-start | bytes 6291460
  11.8 5.5 %collective-permute-start.3 = (bf16[32,1024]{1,0:T(8,128)(2,1)S(1)}, bf16[32,1024]{1,0:T(8,128)(2,1)S(1)}, u32[]{:S(2)}, u32[]{:S(2)}) collective-permute-start(bf16[32,1024]{1,0:T(8,128)(2,1)S(1)} %add.21), channel_id=1, source_target_pairs={{0,12},{4,8},{8,4},{12,0},{16,28},{20,24},{24,20},{28,16},{1,13},{... | collective-permute-start | bytes 196616 | tf_op jit(solution)/shard_map/ppermute | solution.py:25
  14.2 4.3 %collective-permute-start.2 = (bf16[32,1024]{1,0:T(8,128)(2,1)S(1)}, bf16[32,1024]{1,0:T(8,128)(2,1)S(1)}, u32[]{:S(2)}, u32[]{:S(2)}) collective-permute-start(bf16[32,1024]{1,0:T(8,128)(2,1)S(1)} %add.21), channel_id=1, source_target_pairs={{0,8},{4,12},{8,0},{12,4},{16,24},{20,28},{24,16},{28,20},{1,9},{5... | collective-permute-start | bytes 196616 | tf_op jit(solution)/shard_map/ppermute | solution.py:25
  14.9 4.3 %collective-permute-start.1 = (bf16[32,1024]{1,0:T(8,128)(2,1)S(1)}, bf16[32,1024]{1,0:T(8,128)(2,1)S(1)}, u32[]{:S(2)}, u32[]{:S(2)}) collective-permute-start(bf16[32,1024]{1,0:T(8,128)(2,1)S(1)} %add.21), channel_id=1, source_target_pairs={{0,4},{4,0},{8,12},{12,8},{16,20},{20,16},{24,28},{28,24},{1,5},{5... | collective-permute-start | bytes 196616 | tf_op jit(solution)/shard_map/ppermute | solution.py:25
  15.3 17.2 %collective-permute-start.11 = (bf16[256,1024]{1,0:T(8,128)(2,1)S(1)}, bf16[256,1024]{1,0:T(8,128)(2,1)S(1)}, u32[]{:S(2)}, u32[]{:S(2)}) collective-permute-start(bf16[256,1024]{1,0:T(8,128)(2,1)S(1)} %copy-done.9), channel_id=1, source_target_pairs={{0,1},{1,0},{2,3},{3,2},{4,5},{5,4},{6,7},{7,6},{8,9},{9,8},{10,11... | collective-permute-start | bytes 1572872 | tf_op jit(solution)/shard_map/ppermute | solution.py:25
  15.8 16.7 %collective-permute-start.13 = (bf16[256,1024]{1,0:T(8,128)(2,1)S(1)}, bf16[256,1024]{1,0:T(8,128)(2,1)S(1)}, u32[]{:S(2)}, u32[]{:S(2)}) collective-permute-start(bf16[256,1024]{1,0:T(8,128)(2,1)S(1)} %collective-permute-done.12.refs_6_), channel_id=1, source_target_pairs={{0,1},{1,0},{2,3},{3,2},{4,5},{5,4},{6,7},{7,6},{8,9},{9,8},{10,11... | collective-permute-start | bytes 1572872 | tf_op jit(solution)/shard_map/ppermute | solution.py:25
  19.2 1.3 %collective-permute-start.4 = (bf16[32,1024]{1,0:T(8,128)(2,1)S(1)}, bf16[32,1024]{1,0:T(8,128)(2,1)S(1)}, u32[]{:S(2)}, u32[]{:S(2)}) collective-permute-start(bf16[32,1024]{1,0:T(8,128)(2,1)S(1)} %add_add_fusion.own_ref.refs_8_), channel_id=1, source_target_pairs={{0,1},{1,0},{2,3},{3,2},{4,5},{5,4},{6,7},{7,6},{8,9},{9,8},{10,11... | collective-permute-start | bytes 196616 | tf_op jit(solution)/shard_map/ppermute | solution.py:25
  22.6 4.9 %collective-permute-start.7 = (bf16[64,256]{1,0:T(8,128)(2,1)S(1)}, bf16[64,256]{1,0:T(8,128)(2,1)S(1)}, u32[]{:S(2)}, u32[]{:S(2)}) collective-permute-start(bf16[64,256]{1,0:T(8,128)(2,1)S(1)} %get-tuple-element.11), channel_id=1, source_target_pairs={{0,12},{4,8},{8,4},{12,0},{16,28},{20,24},{24,20},{28,16},{1,13},{... | collective-permute-start | bytes 98312 | tf_op jit(solution)/shard_map/ppermute | solution.py:25
  23.9 3.9 %collective-permute-start.6 = (bf16[64,256]{1,0:T(8,128)(2,1)S(1)}, bf16[64,256]{1,0:T(8,128)(2,1)S(1)}, u32[]{:S(2)}, u32[]{:S(2)}) collective-permute-start(bf16[64,256]{1,0:T(8,128)(2,1)S(1)} %get-tuple-element.11), channel_id=1, source_target_pairs={{0,8},{4,12},{8,0},{12,4},{16,24},{20,28},{24,16},{28,20},{1,9},{5... | collective-permute-start | bytes 98312 | tf_op jit(solution)/shard_map/ppermute | solution.py:25
  24.5 3.9 %collective-permute-start.5 = (bf16[64,256]{1,0:T(8,128)(2,1)S(1)}, bf16[64,256]{1,0:T(8,128)(2,1)S(1)}, u32[]{:S(2)}, u32[]{:S(2)}) collective-permute-start(bf16[64,256]{1,0:T(8,128)(2,1)S(1)} %get-tuple-element.11), channel_id=1, source_target_pairs={{0,4},{4,0},{8,12},{12,8},{16,20},{20,16},{24,28},{28,24},{1,5},{5... | collective-permute-start | bytes 98312 | tf_op jit(solution)/shard_map/ppermute | solution.py:25
  28.4 3.4 %collective-permute-start.10 = (bf16[64,256]{1,0:T(8,128)(2,1)S(1)}, bf16[64,256]{1,0:T(8,128)(2,1)S(1)}, u32[]{:S(2)}, u32[]{:S(2)}) collective-permute-start(bf16[64,256]{1,0:T(8,128)(2,1)S(1)} %add_add_fusion.1.refs_0_), channel_id=1, source_target_pairs={{0,3},{1,2},{2,1},{3,0},{4,7},{5,6},{6,5},{7,4},{8,11},{9,10},{10,... | collective-permute-start | bytes 98312 | tf_op jit(solution)/shard_map/ppermute | solution.py:25
  28.5 4.0 %collective-permute-start.9 = (bf16[64,256]{1,0:T(8,128)(2,1)S(1)}, bf16[64,256]{1,0:T(8,128)(2,1)S(1)}, u32[]{:S(2)}, u32[]{:S(2)}) collective-permute-start(bf16[64,256]{1,0:T(8,128)(2,1)S(1)} %add_add_fusion.1.refs_0_), channel_id=1, source_target_pairs={{0,2},{1,3},{2,0},{3,1},{4,6},{5,7},{6,4},{7,5},{8,10},{9,11},{10,... | collective-permute-start | bytes 98312 | tf_op jit(solution)/shard_map/ppermute | solution.py:25
  29.1 3.5 %collective-permute-start.8 = (bf16[64,256]{1,0:T(8,128)(2,1)S(1)}, bf16[64,256]{1,0:T(8,128)(2,1)S(1)}, u32[]{:S(2)}, u32[]{:S(2)}) collective-permute-start(bf16[64,256]{1,0:T(8,128)(2,1)S(1)} %add_add_fusion.1.refs_0_), channel_id=1, source_target_pairs={{0,1},{1,0},{2,3},{3,2},{4,5},{5,4},{6,7},{7,6},{8,9},{9,8},{10,11... | collective-permute-start | bytes 98312 | tf_op jit(solution)/shard_map/ppermute | solution.py:25
  30.4 16.0 %copy-start = (bf16[1024,1024]{1,0:T(8,128)(2,1)S(1)}, bf16[1024,1024]{1,0:T(8,128)(2,1)}, u32[]{:S(2)}) copy-start(bf16[1024,1024]{1,0:T(8,128)(2,1)} %refs_5_.1) | copy-start | bytes 6291460
  34.8 5.3 %collective-permute-start.14 = (bf16[16,1152]{1,0:T(8,128)(2,1)S(1)}, bf16[16,1152]{1,0:T(8,128)(2,1)S(1)}, u32[]{:S(2)}, u32[]{:S(2)}) collective-permute-start(bf16[16,1152]{1,0:T(8,128)(2,1)S(1)} %get-tuple-element.12), channel_id=1, source_target_pairs={{0,12},{4,8},{8,4},{12,0},{16,28},{20,24},{24,20},{28,16},{1,13},{... | collective-permute-start | bytes 110600 | tf_op jit(solution)/shard_map/ppermute | solution.py:25
  37.2 4.0 %collective-permute-start.15 = (bf16[16,1152]{1,0:T(8,128)(2,1)S(1)}, bf16[16,1152]{1,0:T(8,128)(2,1)S(1)}, u32[]{:S(2)}, u32[]{:S(2)}) collective-permute-start(bf16[16,1152]{1,0:T(8,128)(2,1)S(1)} %get-tuple-element.13), channel_id=1, source_target_pairs={{0,8},{4,12},{8,0},{12,4},{16,24},{20,28},{24,16},{28,20},{1,9},{5... | collective-permute-start | bytes 110600 | tf_op jit(solution)/shard_map/ppermute | solution.py:25
  37.9 4.0 %collective-permute-start.16 = (bf16[16,1152]{1,0:T(8,128)(2,1)S(1)}, bf16[16,1152]{1,0:T(8,128)(2,1)S(1)}, u32[]{:S(2)}, u32[]{:S(2)}) collective-permute-start(bf16[16,1152]{1,0:T(8,128)(2,1)S(1)} %get-tuple-element.14), channel_id=1, source_target_pairs={{0,4},{4,0},{8,12},{12,8},{16,20},{20,16},{24,28},{28,24},{1,5},{5... | collective-permute-start | bytes 110600 | tf_op jit(solution)/shard_map/ppermute | solution.py:25
  42.2 3.4 %collective-permute-start.19 = (bf16[16,1152]{1,0:T(8,128)(2,1)S(1)}, bf16[16,1152]{1,0:T(8,128)(2,1)S(1)}, u32[]{:S(2)}, u32[]{:S(2)}) collective-permute-start(bf16[16,1152]{1,0:T(8,128)(2,1)S(1)} %merge.1.refs_0_), channel_id=1, source_target_pairs={{0,3},{1,2},{2,1},{3,0},{4,7},{5,6},{6,5},{7,4},{8,11},{9,10},{10,... | collective-permute-start | bytes 110600 | tf_op jit(solution)/shard_map/ppermute | solution.py:25
  42.2 4.2 %collective-permute-start.18 = (bf16[16,1152]{1,0:T(8,128)(2,1)S(1)}, bf16[16,1152]{1,0:T(8,128)(2,1)S(1)}, u32[]{:S(2)}, u32[]{:S(2)}) collective-permute-start(bf16[16,1152]{1,0:T(8,128)(2,1)S(1)} %merge.1.refs_0_), channel_id=1, source_target_pairs={{0,2},{1,3},{2,0},{3,1},{4,6},{5,7},{6,4},{7,5},{8,10},{9,11},{10,... | collective-permute-start | bytes 110600 | tf_op jit(solution)/shard_map/ppermute | solution.py:25
  42.8 3.6 %collective-permute-start.17 = (bf16[16,1152]{1,0:T(8,128)(2,1)S(1)}, bf16[16,1152]{1,0:T(8,128)(2,1)S(1)}, u32[]{:S(2)}, u32[]{:S(2)}) collective-permute-start(bf16[16,1152]{1,0:T(8,128)(2,1)S(1)} %merge.1.refs_0_), channel_id=1, source_target_pairs={{0,1},{1,0},{2,3},{3,2},{4,5},{5,4},{6,7},{7,6},{8,9},{9,8},{10,11... | collective-permute-start | bytes 110600 | tf_op jit(solution)/shard_map/ppermute | solution.py:25

commit v3 on v2

--- a/solution.py
+++ b/solution.py
@@ -25,6 +25,13 @@
     return lax.ppermute(value, axis, pairs)
 
 
+def cross(value, mask):
+    patches = lax.axis_size("patch")
+    devices = lax.axis_size("dp") * patches
+    pairs = [(source, source ^ (mask * patches + 1)) for source in range(devices)]
+    return lax.ppermute(value, ("dp", "patch"), pairs)
+
+
 def params(mib):
     return pltpu.CompilerParams(vmem_limit_bytes=mib * 2**20)
 
@@ -50,7 +57,7 @@
 def join_halves(own_ref, other_ref, core):
     own = own_ref[...].astype(f32)
     other = other_ref[...].astype(f32)
-    return jnp.concatenate([jnp.where(core == 0, own, other), jnp.where(core == 0, other, own)], 0)
+    return jnp.concatenate([jnp.where(core == 1, own, other), jnp.where(core == 1, other, own)], 0)
 
 
 def gather_kernel(ids_ref, table_ref, *refs, slots, images, slab):
@@ -122,7 +129,11 @@
         mine = pl.ds(beam, images, stride=BEAMS)
         key_ref[:, first : first + LANES] = key_scr[first // LANES, mine, :].astype(bf16)
         value_ref[:, first : first + LANES] = value_scr[first // LANES, mine, :].astype(bf16)
-    sub = lax.broadcasted_iota(jnp.int32, (SUB, width), 0)
+    shape = (BEAMS * images, parents_ref.shape[1])
+    row = lax.broadcasted_iota(jnp.int32, shape, 0)
+    row = (group * BEAMS + row % BEAMS) * images + row // BEAMS
+    chosen = jnp.logical_and(row == lax.broadcasted_iota(jnp.int32, shape, 1), parents_ref[...] == beam)
+    lives = jnp.sum(chosen.astype(f32), axis=-1, keepdims=True)
     pairs = images // PAIR
     seen = same_image((heads * SUB, PAIR * length), length)
     scores, owns = [], []
@@ -147,11 +158,7 @@
         v = jnp.concatenate([values[j * SUB : (j + 1) * SUB]] * heads, 0)
         summed = (dot(weights[j], past) + own_weights[j] * v) / totals[j]
         folded = fold(summed, heads, head_size)
-        lives = jnp.zeros((SUB, width), jnp.int32)
-        for k in range(SUB):
-            row = (group * BEAMS + k % BEAMS) * images + j * PAIR + k // BEAMS
-            lives = jnp.where(sub == k, (parents_ref[row] == beam).astype(jnp.int32), lives)
-        done.append(jnp.where(lives > 0, folded, 0.0))
+        done.append(jnp.where(lives[j * SUB : (j + 1) * SUB] > 0.5, folded, 0.0))
     context_ref[...] = jnp.concatenate(done, 0).astype(bf16)
 
 
@@ -304,7 +311,6 @@
     patches = lax.axis_size("patch")
     group_rows = BEAMS * images
     half = group_rows // 2
-    smem = pl.BlockSpec(memory_space=pltpu.SMEM)
     vmem = pl.BlockSpec(memory_space=pltpu.VMEM)
 
     weights = {0: output_weight}
@@ -342,26 +348,26 @@
         keep = len(slots) // 2
         slots = [a + swap(b, "dp", keep * BEAMS) for a, b in zip(slots[:keep], slots[keep:])]
     own = slots[0]
-    own = own + sum(swap(own, "dp", k) for k in range(1, BEAMS))
+    own = sum(cross(own, k) for k in range(BEAMS))
     other = swap(own, "patch", 1)
     weights |= {k ^ 1: swap(piece, "patch", 1) for k, piece in weights.items()}
-    outputs = [weights[k] for k in range(patches)]
+    outputs = [weights[k ^ 1] for k in range(patches)]
 
     context, new_key, new_value = pl.pallas_call(
         functools.partial(self_kernel, head_size=head_size),
         out_shape=[
             jax.ShapeDtypeStruct((group_rows, width_here), bf16),
-            jax.ShapeDtypeStruct((images, width_here), bf16),
-            jax.ShapeDtypeStruct((images, width_here), bf16),
+            pltpu.VMEM((images, width_here), bf16),
+            pltpu.VMEM((images, width_here), bf16),
         ],
-        in_specs=[smem] + [vmem] * 8,
+        in_specs=[vmem] * 9,
         out_specs=[vmem] * 3,
         scratch_shapes=[pltpu.VMEM((width_here // LANES, group_rows, LANES), f32)] * 2,
         compiler_params=params(16),
         name="self_attention",
-    )(parents, own, other, self_gain.reshape(1, width), query_weight, key_weight, value_weight,
+    )(parents.reshape(1, -1), own, other, self_gain.reshape(1, width), query_weight, key_weight, value_weight,
       past_keys, past_values)
-    context = context + sum(swap(context, "dp", k) for k in range(1, BEAMS))
+    context = sum(cross(context, k) for k in range(BEAMS))
     contexts = [context] + [swap(context, "patch", k) for k in range(1, patches)]
 
     patch_count = image_keys.shape[2]
@@ -382,7 +388,7 @@
         name="cross_attention",
     )(*contexts, *outputs, own, other, cross_gain.reshape(1, width), cross_query, image_keys,
       image_values)
-    parts = [swap(messages[k], "dp", k) for k in range(BEAMS - 1, 0, -1)] + [messages[0]]
+    parts = [cross(messages[k], k) for k in range(BEAMS - 1, 0, -1)] + [messages[0]]
     part = pl.pallas_call(
         functools.partial(merge_kernel, head_size=head_size),
         out_shape=jax.ShapeDtypeStruct((images, width + LANES), bf16),

time: 48.1 us -> 46.4 us (0.965)
  local copies, waits for them, and re-layouts: 0.09 us -> 1.28 us
  Pallas kernels: 11 us -> 9.97 us
  starting transfers between devices: 20.1 us -> 19.1 us
  waiting for transfers between devices: 15.5 us -> 14.7 us
    ppermute x20 -> x11, waiting for transfers between devices: 15.5 us -> 5.48 us  [swap(): return lax.ppermute(value, axis, pairs)]
    ppermute x20 -> x11, starting transfers between devices: 20.1 us -> 10.1 us  [swap(): return lax.ppermute(value, axis, pairs)]
    ppermute x0 -> x11, waiting for transfers between devices: none -> 9.26 us  [cross(): return lax.ppermute(value, ('dp', 'patch'), pairs)]
    ppermute x0 -> x11, starting transfers between devices: none -> 9 us  [cross(): return lax.ppermute(value, ('dp', 'patch'), pairs)]
    unnamed x26 -> x28, local copies, waits for them, and re-layouts: 0.08 us -> 1.27 us
    pallas_call x1, Pallas kernels: 2.06 us -> 1 us  [step(): pl.pallas_call(functools.partial(self_kernel, head_size=head_size), out_s...]
  transfers between devices with their start and end apart: 20 -> 22, of which waited for: 16 -> 15; matrix products, arithmetic and copies ran while one was open for 0% -> 3% of each run, Pallas kernels for 15% -> 13%
where the time goes in v3:
time: 46.4 us; the launch traced here: 46 us
  starting transfers between devices  19.1 us (41%)
  waiting for transfers between devices  14.7 us (32%)
  Pallas kernels  9.97 us (21%)
  local copies, waits for them, and re-layouts  1.28 us (3%)
  between operations  0.84 us (2%)
    ppermute x11, starting transfers between devices, swap(): return lax.ppermute(value, axis, pairs)  10.1 us
    ppermute x11, waiting for transfers between devices, cross(): return lax.ppermute(value, ('dp', 'patch'), pairs)  9.26 us
    ppermute x11, starting transfers between devices, cross(): return lax.ppermute(value, ('dp', 'patch'), pairs)  9 us
    ppermute x11, waiting for transfers between devices, swap(): return lax.ppermute(value, axis, pairs)  5.48 us
    pallas_call x2, Pallas kernels, gather(): pl.pallas_call(functools.partial(gather_kernel, slots=slots, images=image...  5.16 us
    pallas_call x1, Pallas kernels, step(): pl.pallas_call(functools.partial(cross_kernel, pieces=patches, head_size=...  2.2 us
    pallas_call x1, Pallas kernels, step(): pl.pallas_call(functools.partial(final_kernel, head_size=head_size), out_...  1.3 us
    unnamed x28, local copies, waits for them, and re-layouts  1.27 us
  transfers between devices with their start and end apart: 22, of which 15 were waited for; matrix products, arithmetic and copies ran while one was open for 3% of the time, Pallas kernels for 13%

profile of v3, /device:TPU:0, one launch (start us, length us, event | category | flops | bytes accessed | tf_op | source)
XLA Modules:
  0.0 46.0 jit_solution(3783625299417668574)
XLA Ops:
  0.6 3.1 %collective-permute-start.14 = (bf16[256,1024]{1,0:T(8,128)(2,1)}, bf16[256,1024]{1,0:T(8,128)(2,1)S(1)}, u32[]{:S(2)}, u32[]{:S(2)}) collective-permute-start(bf16[256,1024]{1,0:T(8,128)(2,1)} %refs_5_.2), channel_id=1, source_target_pairs={{0,2},{1,3},{2,0},{3,1},{4,6},{5,7},{6,4},{7,5},{8,10},{9,11},{10,... | collective-permute-start | bytes 1572872 | tf_op jit(solution)/shard_map/ppermute | solution.py:25
  3.7 2.5 %shard_map.167 = bf16[32,1024]{1,0:T(8,128)(2,1)S(1)} custom-call(s32[128]{0:T(128)} %ids_ref.3, bf16[500,8,1024]{2,1,0:T(8,128)(2,1)} %bitcast.3), custom_call_target="tpu_custom_call" | custom-call | tf_op jit(solution)/shard_map/pallas_call | solution.py:327
  6.2 0.0 copy-start.9
  6.3 0.0 copy-start.5
  6.3 0.0 copy-start.6
  6.3 2.6 %collective-permute-start = (bf16[32,1024]{1,0:T(8,128)(2,1)S(1)}, bf16[32,1024]{1,0:T(8,128)(2,1)S(1)}, u32[]{:S(2)}, u32[]{:S(2)}) collective-permute-start(bf16[32,1024]{1,0:T(8,128)(2,1)S(1)} %shard_map.167), channel_id=1, source_target_pairs={{0,16},{4,20},{8,24},{12,28},{16,0},{20,4},{24,8},{28,12},{1,17},{... | collective-permute-start | bytes 196616 | tf_op jit(solution)/shard_map/ppermute | solution.py:25
  8.9 2.6 %shard_map.166 = bf16[32,1024]{1,0:T(8,128)(2,1)S(1)} custom-call(s32[128]{0:T(128)} %ids_ref.3, bf16[500,8,1024]{2,1,0:T(8,128)(2,1)} %bitcast.4), custom_call_target="tpu_custom_call" | custom-call | tf_op jit(solution)/shard_map/pallas_call | solution.py:327
  11.5 0.2 collective-permute-done
  11.8 1.4 %collective-permute-start.4 = (bf16[32,1024]{1,0:T(8,128)(2,1)S(1)}, bf16[32,1024]{1,0:T(8,128)(2,1)S(1)}, u32[]{:S(2)}, u32[]{:S(2)}) collective-permute-start(bf16[32,1024]{1,0:T(8,128)(2,1)S(1)} %add.21), channel_id=1, source_target_pairs={{0,13},{1,12},{2,15},{3,14},{4,9},{5,8},{6,11},{7,10},{8,5},{9,4},... | collective-permute-start | bytes 196616 | tf_op jit(solution)/shard_map/ppermute | solution.py:32
  13.1 1.5 %collective-permute-start.3 = (bf16[32,1024]{1,0:T(8,128)(2,1)S(1)}, bf16[32,1024]{1,0:T(8,128)(2,1)S(1)}, u32[]{:S(2)}, u32[]{:S(2)}) collective-permute-start(bf16[32,1024]{1,0:T(8,128)(2,1)S(1)} %add.21), channel_id=1, source_target_pairs={{0,9},{1,8},{2,11},{3,10},{4,13},{5,12},{6,15},{7,14},{8,1},{9,0},... | collective-permute-start | bytes 196616 | tf_op jit(solution)/shard_map/ppermute | solution.py:32
  14.6 0.0 collective-permute-start.2
  14.6 0.6 %collective-permute-start.1 = (bf16[32,1024]{1,0:T(8,128)(2,1)S(1)}, bf16[32,1024]{1,0:T(8,128)(2,1)S(1)}, u32[]{:S(2)}, u32[]{:S(2)}) collective-permute-start(bf16[32,1024]{1,0:T(8,128)(2,1)S(1)} %add.21), channel_id=1, source_target_pairs={{0,1},{1,0},{2,3},{3,2},{4,5},{5,4},{6,7},{7,6},{8,9},{9,8},{10,11... | collective-permute-start | bytes 196616 | tf_op jit(solution)/shard_map/ppermute | solution.py:32
  15.2 1.9 %collective-permute-done.4 = bf16[32,1024]{1,0:T(8,128)(2,1)S(1)} collective-permute-done((bf16[32,1024]{1,0:T(8,128)(2,1)S(1)}, bf16[32,1024]{1,0:T(8,128)(2,1)S(1)}, u32[]{:S(2)}, u32[]{:S(2)}) %collective-permute-start.4) | collective-permute-done | bytes 65568 | tf_op jit(solution)/shard_map/ppermute | solution.py:32
  17.1 0.1 collective-permute-start.13
  17.2 0.4 collective-permute-start.15
  17.6 1.4 %collective-permute-done.2 = bf16[32,1024]{1,0:T(8,128)(2,1)S(1)} collective-permute-done((bf16[32,1024]{1,0:T(8,128)(2,1)S(1)}, bf16[32,1024]{1,0:T(8,128)(2,1)S(1)}, u32[]{:S(2)}, u32[]{:S(2)}) %collective-permute-start.2) | collective-permute-done | bytes 65568 | tf_op jit(solution)/shard_map/ppermute | solution.py:32
  18.9 0.1 collective-permute-start.5
  19.1 1.2 %collective-permute-done.5.other_ref.refs_9_ = bf16[32,1024]{1,0:T(8,128)(2,1)S(1)} collective-permute-done((bf16[32,1024]{1,0:T(8,128)(2,1)S(1)}, bf16[32,1024]{1,0:T(8,128)(2,1)S(1)}, u32[]{:S(2)}, u32[]{:S(2)}) %collective-permute-start.5) | collective-permute-done | bytes 65568 | tf_op jit(solution)/shard_map/ppermute | solution.py:25
  20.3 1.0 %self_attention.1 = (bf16[64,256]{1,0:T(8,128)(2,1)S(1)}, bf16[16,256]{1,0:T(8,128)(2,1)S(1)}, bf16[16,256]{1,0:T(8,128)(2,1)S(1)}) custom-call(s32[1,128]{1,0:T(1,128)S(1)} %bitcast.2, bf16[32,1024]{1,0:T(8,128)(2,1)S(1)} %add_add_fusion.own_ref.refs_8_, bf16[32,1024]{1,0:T(8,128)(2,1)S(1)} %collective-permute-done.5.other_ref.refs_9_, ...), custom_call_target="tpu_custom_call" | custom-call | tf_op jit(solution)/shard_map/self_attention/pallas_call | solution.py:356
  21.3 1.3 %collective-permute-start.9 = (bf16[64,256]{1,0:T(8,128)(2,1)S(1)}, bf16[64,256]{1,0:T(8,128)(2,1)S(1)}, u32[]{:S(2)}, u32[]{:S(2)}) collective-permute-start(bf16[64,256]{1,0:T(8,128)(2,1)S(1)} %get-tuple-element.11), channel_id=1, source_target_pairs={{0,13},{1,12},{2,15},{3,14},{4,9},{5,8},{6,11},{7,10},{8,5},{9,4},... | collective-permute-start | bytes 98312 | tf_op jit(solution)/shard_map/ppermute | solution.py:32
  22.6 0.4 collective-permute-start.8
  23.1 1.3 %collective-permute-start.7 = (bf16[64,256]{1,0:T(8,128)(2,1)S(1)}, bf16[64,256]{1,0:T(8,128)(2,1)S(1)}, u32[]{:S(2)}, u32[]{:S(2)}) collective-permute-start(bf16[64,256]{1,0:T(8,128)(2,1)S(1)} %get-tuple-element.11), channel_id=1, source_target_pairs={{0,5},{1,4},{2,7},{3,6},{4,1},{5,0},{6,3},{7,2},{8,13},{9,12},{10,... | collective-permute-start | bytes 98312 | tf_op jit(solution)/shard_map/ppermute | solution.py:32
  24.4 1.3 %collective-permute-done.9 = bf16[64,256]{1,0:T(8,128)(2,1)S(1)} collective-permute-done((bf16[64,256]{1,0:T(8,128)(2,1)S(1)}, bf16[64,256]{1,0:T(8,128)(2,1)S(1)}, u32[]{:S(2)}, u32[]{:S(2)}) %collective-permute-start.9) | collective-permute-done | bytes 32800 | tf_op jit(solution)/shard_map/ppermute | solution.py:32
  25.6 0.2 collective-permute-start.6
  25.8 0.1 collective-permute-done.8
  26.0 0.5 %collective-permute-done.7 = bf16[64,256]{1,0:T(8,128)(2,1)S(1)} collective-permute-done((bf16[64,256]{1,0:T(8,128)(2,1)S(1)}, bf16[64,256]{1,0:T(8,128)(2,1)S(1)}, u32[]{:S(2)}, u32[]{:S(2)}) %collective-permute-start.7) | collective-permute-done | bytes 32800 | tf_op jit(solution)/shard_map/ppermute | solution.py:32
  26.4 0.4 collective-permute-done.6
  26.9 0.4 collective-permute-start.12
  27.2 1.5 %collective-permute-start.11 = (bf16[64,256]{1,0:T(8,128)(2,1)S(1)}, bf16[64,256]{1,0:T(8,128)(2,1)S(1)}, u32[]{:S(2)}, u32[]{:S(2)}) collective-permute-start(bf16[64,256]{1,0:T(8,128)(2,1)S(1)} %add_add_fusion.1.refs_0_), channel_id=1, source_target_pairs={{0,2},{1,3},{2,0},{3,1},{4,6},{5,7},{6,4},{7,5},{8,10},{9,11},{10,... | collective-permute-start | bytes 98312 | tf_op jit(solution)/shard_map/ppermute | solution.py:25
  28.7 0.0 collective-permute-start.10
  28.8 1.5 %collective-permute-done.12.refs_3_ = bf16[64,256]{1,0:T(8,128)(2,1)S(1)} collective-permute-done((bf16[64,256]{1,0:T(8,128)(2,1)S(1)}, bf16[64,256]{1,0:T(8,128)(2,1)S(1)}, u32[]{:S(2)}, u32[]{:S(2)}) %collective-permute-start.12) | collective-permute-done | bytes 32800 | tf_op jit(solution)/shard_map/ppermute | solution.py:25
  30.3 1.1 %collective-permute-done.11.refs_2_ = bf16[64,256]{1,0:T(8,128)(2,1)S(1)} collective-permute-done((bf16[64,256]{1,0:T(8,128)(2,1)S(1)}, bf16[64,256]{1,0:T(8,128)(2,1)S(1)}, u32[]{:S(2)}, u32[]{:S(2)}) %collective-permute-start.11) | collective-permute-done | bytes 32800 | tf_op jit(solution)/shard_map/ppermute | solution.py:25
  31.4 2.2 %cross_attention.1 = (f32[16,1024]{1,0:T(8,128)S(1)}, bf16[16,1152]{1,0:T(8,128)(2,1)S(1)}, bf16[16,1152]{1,0:T(8,128)(2,1)S(1)}, bf16[16,1152]{1,0:T(8,128)(2,1)S(1)}, bf16[16,1152]{1,0:T(8,128)(2,1)S(1)}) custom-call(bf16[64,256]{1,0:T(8,128)(2,1)S(1)} %add_add_fusion.1.refs_0_, bf16[64,256]{1,0:T(8,128)(2,1)S(1)} %collective-permute-done.10.refs_1_, ...), custom_call_target="tpu_custom_call" | custom-call | tf_op jit(solution)/shard_map/cross_attention/pallas_call | solution.py:375
  33.6 0.8 %collective-permute-start.16 = (bf16[16,1152]{1,0:T(8,128)(2,1)S(1)}, bf16[16,1152]{1,0:T(8,128)(2,1)S(1)}, u32[]{:S(2)}, u32[]{:S(2)}) collective-permute-start(bf16[16,1152]{1,0:T(8,128)(2,1)S(1)} %get-tuple-element.12), channel_id=1, source_target_pairs={{0,13},{1,12},{2,15},{3,14},{4,9},{5,8},{6,11},{7,10},{8,5},{9,4},... | collective-permute-start | bytes 110600 | tf_op jit(solution)/shard_map/ppermute | solution.py:32
  34.3 1.6 %collective-permute-start.17 = (bf16[16,1152]{1,0:T(8,128)(2,1)S(1)}, bf16[16,1152]{1,0:T(8,128)(2,1)S(1)}, u32[]{:S(2)}, u32[]{:S(2)}) collective-permute-start(bf16[16,1152]{1,0:T(8,128)(2,1)S(1)} %get-tuple-element.13), channel_id=1, source_target_pairs={{0,9},{1,8},{2,11},{3,10},{4,13},{5,12},{6,15},{7,14},{8,1},{9,0},... | collective-permute-start | bytes 110600 | tf_op jit(solution)/shard_map/ppermute | solution.py:32
  35.9 0.0 collective-permute-start.18
  36.0 2.0 %collective-permute-done.16.refs_0_ = bf16[16,1152]{1,0:T(8,128)(2,1)S(1)} collective-permute-done((bf16[16,1152]{1,0:T(8,128)(2,1)S(1)}, bf16[16,1152]{1,0:T(8,128)(2,1)S(1)}, u32[]{:S(2)}, u32[]{:S(2)}) %collective-permute-start.16) | collective-permute-done | bytes 36896 | tf_op jit(solution)/shard_map/ppermute | solution.py:32
  38.0 0.3 collective-permute-done.17.refs_1_
  38.3 1.4 %collective-permute-done.18.refs_2_ = bf16[16,1152]{1,0:T(8,128)(2,1)S(1)} collective-permute-done((bf16[16,1152]{1,0:T(8,128)(2,1)S(1)}, bf16[16,1152]{1,0:T(8,128)(2,1)S(1)}, u32[]{:S(2)}, u32[]{:S(2)}) %collective-permute-start.18) | collective-permute-done | bytes 36896 | tf_op jit(solution)/shard_map/ppermute | solution.py:32
  39.7 0.3 merge.1.refs_0_
  40.0 0.7 %collective-permute-start.21 = (bf16[16,1152]{1,0:T(8,128)(2,1)S(1)}, bf16[16,1152]{1,0:T(8,128)(2,1)S(1)}, u32[]{:S(2)}, u32[]{:S(2)}) collective-permute-start(bf16[16,1152]{1,0:T(8,128)(2,1)S(1)} %merge.1.refs_0_), channel_id=1, source_target_pairs={{0,3},{1,2},{2,1},{3,0},{4,7},{5,6},{6,5},{7,4},{8,11},{9,10},{10,... | collective-permute-start | bytes 110600 | tf_op jit(solution)/shard_map/ppermute | solution.py:25
  40.7 1.0 %collective-permute-start.20 = (bf16[16,1152]{1,0:T(8,128)(2,1)S(1)}, bf16[16,1152]{1,0:T(8,128)(2,1)S(1)}, u32[]{:S(2)}, u32[]{:S(2)}) collective-permute-start(bf16[16,1152]{1,0:T(8,128)(2,1)S(1)} %merge.1.refs_0_), channel_id=1, source_target_pairs={{0,2},{1,3},{2,0},{3,1},{4,6},{5,7},{6,4},{7,5},{8,10},{9,11},{10,... | collective-permute-start | bytes 110600 | tf_op jit(solution)/shard_map/ppermute | solution.py:25
  41.7 0.2 collective-permute-start.19
  41.9 0.6 %copy.18 = bf16[16,256]{1,0:T(8,128)(2,1)} copy(bf16[16,256]{1,0:T(8,128)(2,1)S(1)} %get-tuple-element.20) | data formatting | bytes 16384
  42.5 0.6 %copy.19 = bf16[16,256]{1,0:T(8,128)(2,1)} copy(bf16[16,256]{1,0:T(8,128)(2,1)S(1)} %get-tuple-element.21) | data formatting | bytes 16384
  43.1 0.5 %collective-permute-done.21.refs_3_ = bf16[16,1152]{1,0:T(8,128)(2,1)S(1)} collective-permute-done((bf16[16,1152]{1,0:T(8,128)(2,1)S(1)}, bf16[16,1152]{1,0:T(8,128)(2,1)S(1)}, u32[]{:S(2)}, u32[]{:S(2)}) %collective-permute-start.21) | collective-permute-done | bytes 36896 | tf_op jit(solution)/shard_map/ppermute | solution.py:25
  43.6 1.1 %collective-permute-done.20.refs_2_ = bf16[16,1152]{1,0:T(8,128)(2,1)S(1)} collective-permute-done((bf16[16,1152]{1,0:T(8,128)(2,1)S(1)}, bf16[16,1152]{1,0:T(8,128)(2,1)S(1)}, u32[]{:S(2)}, u32[]{:S(2)}) %collective-permute-start.20) | collective-permute-done | bytes 36896 | tf_op jit(solution)/shard_map/ppermute | solution.py:25
  44.7 1.3 %final.1 = bf16[16,1024]{1,0:T(8,128)(2,1)} custom-call(bf16[16,1152]{1,0:T(8,128)(2,1)S(1)} %merge.1.refs_0_, bf16[16,1152]{1,0:T(8,128)(2,1)S(1)} %collective-permute-done.19.refs_1_, bf16[16,1152]{1,0:T(8,128)(2,1)S(1)} %collective-permute-done.20.refs_2_, bf16[16,1152]{1,0:T(8,128)(2,1)S(1)} %collective-permute-done.21.refs_3_, ...), custom_call_target="tpu_custom_call" | custom-call | tf_op jit(solution)/shard_map/final/pallas_call | solution.py:401
  (35 shorter events, 0.1 us)
Async XLA Ops:
  0.6 16.5 %collective-permute-start.14 = (bf16[256,1024]{1,0:T(8,128)(2,1)}, bf16[256,1024]{1,0:T(8,128)(2,1)S(1)}, u32[]{:S(2)}, u32[]{:S(2)}) collective-permute-start(bf16[256,1024]{1,0:T(8,128)(2,1)} %refs_5_.2), channel_id=1, source_target_pairs={{0,2},{1,3},{2,0},{3,1},{4,6},{5,7},{6,4},{7,5},{8,10},{9,11},{10,... | collective-permute-start | bytes 1572872 | tf_op jit(solution)/shard_map/ppermute | solution.py:25
  6.2 10.8 %copy-start.9 = (bf16[256,1024]{1,0:T(8,128)(2,1)S(1)}, bf16[256,1024]{1,0:T(8,128)(2,1)}, u32[]{:S(2)}) copy-start(bf16[256,1024]{1,0:T(8,128)(2,1)} %refs_5_.2) | copy-start | bytes 1572868
  6.2 12.8 %copy-start.11 = (bf16[1024]{0:T(1024)(128)(2,1)S(1)}, bf16[1024]{0:T(1024)(128)(2,1)}, u32[]{:S(2)}) copy-start(bf16[1024]{0:T(1024)(128)(2,1)} %param.18) | copy-start | bytes 6148
  6.3 14.0 %copy-start.4 = (bf16[16,128,256]{2,1,0:T(8,128)(2,1)S(1)}, bf16[16,128,256]{2,1,0:T(8,128)(2,1)}, u32[]{:S(2)}) copy-start(bf16[16,128,256]{2,1,0:T(8,128)(2,1)} %pk_ref.1) | copy-start | bytes 3145732
  6.3 14.0 %copy-start.5 = (bf16[16,128,256]{2,1,0:T(8,128)(2,1)S(1)}, bf16[16,128,256]{2,1,0:T(8,128)(2,1)}, u32[]{:S(2)}) copy-start(bf16[16,128,256]{2,1,0:T(8,128)(2,1)} %pv_ref.1) | copy-start | bytes 3145732
  6.3 14.0 %copy-start.6 = (bf16[1024,256]{1,0:T(8,128)(2,1)S(1)}, bf16[1024,256]{1,0:T(8,128)(2,1)}, u32[]{:S(2)}) copy-start(bf16[1024,256]{1,0:T(8,128)(2,1)} %wq_ref.1) | copy-start | bytes 1572868
  6.3 14.0 %copy-start.7 = (bf16[1024,256]{1,0:T(8,128)(2,1)S(1)}, bf16[1024,256]{1,0:T(8,128)(2,1)}, u32[]{:S(2)}) copy-start(bf16[1024,256]{1,0:T(8,128)(2,1)} %wk_ref.1) | copy-start | bytes 1572868
  6.3 14.0 %copy-start.8 = (bf16[1024,256]{1,0:T(8,128)(2,1)S(1)}, bf16[1024,256]{1,0:T(8,128)(2,1)}, u32[]{:S(2)}) copy-start(bf16[1024,256]{1,0:T(8,128)(2,1)} %wv_ref.1) | copy-start | bytes 1572868
  6.3 14.0 %copy-start.10 = (s32[128]{0:T(128)S(1)}, s32[128]{0:T(128)}, u32[]{:S(2)}) copy-start(s32[128]{0:T(128)} %param.16) | copy-start | bytes 1540
  6.3 5.4 %collective-permute-start = (bf16[32,1024]{1,0:T(8,128)(2,1)S(1)}, bf16[32,1024]{1,0:T(8,128)(2,1)S(1)}, u32[]{:S(2)}, u32[]{:S(2)}) collective-permute-start(bf16[32,1024]{1,0:T(8,128)(2,1)S(1)} %shard_map.167), channel_id=1, source_target_pairs={{0,16},{4,20},{8,24},{12,28},{16,0},{20,4},{24,8},{28,12},{1,17},{... | collective-permute-start | bytes 196616 | tf_op jit(solution)/shard_map/ppermute | solution.py:25
  8.9 22.5 %copy-start.3 = (bf16[1,16,64,1024]{3,2,1,0:T(8,128)(2,1)S(1)}, bf16[1,16,64,1024]{3,2,1,0:T(8,128)(2,1)}, u32[]{:S(2)}) copy-start(bf16[1,16,64,1024]{3,2,1,0:T(8,128)(2,1)} %refs_13_.1) | copy-start | bytes 6291460
  11.7 17.1 %copy-start.12 = (bf16[1024]{0:T(1024)(128)(2,1)S(1)}, bf16[1024]{0:T(1024)(128)(2,1)}, u32[]{:S(2)}) copy-start(bf16[1024]{0:T(1024)(128)(2,1)} %param.25) | copy-start | bytes 6148
  11.7 19.6 %copy-start.1 = (bf16[1024,1024]{1,0:T(8,128)(2,1)S(1)}, bf16[1024,1024]{1,0:T(8,128)(2,1)}, u32[]{:S(2)}) copy-start(bf16[1024,1024]{1,0:T(8,128)(2,1)} %refs_11_.1) | copy-start | bytes 6291460
  11.7 19.6 %copy-start.2 = (bf16[1,16,64,1024]{3,2,1,0:T(8,128)(2,1)S(1)}, bf16[1,16,64,1024]{3,2,1,0:T(8,128)(2,1)}, u32[]{:S(2)}) copy-start(bf16[1,16,64,1024]{3,2,1,0:T(8,128)(2,1)} %refs_12_.1) | copy-start | bytes 6291460
  11.8 5.3 %collective-permute-start.4 = (bf16[32,1024]{1,0:T(8,128)(2,1)S(1)}, bf16[32,1024]{1,0:T(8,128)(2,1)S(1)}, u32[]{:S(2)}, u32[]{:S(2)}) collective-permute-start(bf16[32,1024]{1,0:T(8,128)(2,1)S(1)} %add.21), channel_id=1, source_target_pairs={{0,13},{1,12},{2,15},{3,14},{4,9},{5,8},{6,11},{7,10},{8,5},{9,4},... | collective-permute-start | bytes 196616 | tf_op jit(solution)/shard_map/ppermute | solution.py:32
  13.1 4.4 %collective-permute-start.3 = (bf16[32,1024]{1,0:T(8,128)(2,1)S(1)}, bf16[32,1024]{1,0:T(8,128)(2,1)S(1)}, u32[]{:S(2)}, u32[]{:S(2)}) collective-permute-start(bf16[32,1024]{1,0:T(8,128)(2,1)S(1)} %add.21), channel_id=1, source_target_pairs={{0,9},{1,8},{2,11},{3,10},{4,13},{5,12},{6,15},{7,14},{8,1},{9,0},... | collective-permute-start | bytes 196616 | tf_op jit(solution)/shard_map/ppermute | solution.py:32
  14.6 4.3 %collective-permute-start.2 = (bf16[32,1024]{1,0:T(8,128)(2,1)S(1)}, bf16[32,1024]{1,0:T(8,128)(2,1)S(1)}, u32[]{:S(2)}, u32[]{:S(2)}) collective-permute-start(bf16[32,1024]{1,0:T(8,128)(2,1)S(1)} %add.21), channel_id=1, source_target_pairs={{0,5},{1,4},{2,7},{3,6},{4,1},{5,0},{6,3},{7,2},{8,13},{9,12},{10,... | collective-permute-start | bytes 196616 | tf_op jit(solution)/shard_map/ppermute | solution.py:32
  14.6 4.3 %collective-permute-start.1 = (bf16[32,1024]{1,0:T(8,128)(2,1)S(1)}, bf16[32,1024]{1,0:T(8,128)(2,1)S(1)}, u32[]{:S(2)}, u32[]{:S(2)}) collective-permute-start(bf16[32,1024]{1,0:T(8,128)(2,1)S(1)} %add.21), channel_id=1, source_target_pairs={{0,1},{1,0},{2,3},{3,2},{4,5},{5,4},{6,7},{7,6},{8,9},{9,8},{10,11... | collective-permute-start | bytes 196616 | tf_op jit(solution)/shard_map/ppermute | solution.py:32
  17.1 14.3 %collective-permute-start.13 = (bf16[256,1024]{1,0:T(8,128)(2,1)S(1)}, bf16[256,1024]{1,0:T(8,128)(2,1)S(1)}, u32[]{:S(2)}, u32[]{:S(2)}) collective-permute-start(bf16[256,1024]{1,0:T(8,128)(2,1)S(1)} %copy-done.9), channel_id=1, source_target_pairs={{0,1},{1,0},{2,3},{3,2},{4,5},{5,4},{6,7},{7,6},{8,9},{9,8},{10,11... | collective-permute-start | bytes 1572872 | tf_op jit(solution)/shard_map/ppermute | solution.py:25
  17.2 14.2 %collective-permute-start.15 = (bf16[256,1024]{1,0:T(8,128)(2,1)S(1)}, bf16[256,1024]{1,0:T(8,128)(2,1)S(1)}, u32[]{:S(2)}, u32[]{:S(2)}) collective-permute-start(bf16[256,1024]{1,0:T(8,128)(2,1)S(1)} %collective-permute-done.14.refs_7_), channel_id=1, source_target_pairs={{0,1},{1,0},{2,3},{3,2},{4,5},{5,4},{6,7},{7,6},{8,9},{9,8},{10,11... | collective-permute-start | bytes 1572872 | tf_op jit(solution)/shard_map/ppermute | solution.py:25
  18.9 1.3 %collective-permute-start.5 = (bf16[32,1024]{1,0:T(8,128)(2,1)S(1)}, bf16[32,1024]{1,0:T(8,128)(2,1)S(1)}, u32[]{:S(2)}, u32[]{:S(2)}) collective-permute-start(bf16[32,1024]{1,0:T(8,128)(2,1)S(1)} %add_add_fusion.own_ref.refs_8_), channel_id=1, source_target_pairs={{0,1},{1,0},{2,3},{3,2},{4,5},{5,4},{6,7},{7,6},{8,9},{9,8},{10,11... | collective-permute-start | bytes 196616 | tf_op jit(solution)/shard_map/ppermute | solution.py:25
  21.3 4.3 %collective-permute-start.9 = (bf16[64,256]{1,0:T(8,128)(2,1)S(1)}, bf16[64,256]{1,0:T(8,128)(2,1)S(1)}, u32[]{:S(2)}, u32[]{:S(2)}) collective-permute-start(bf16[64,256]{1,0:T(8,128)(2,1)S(1)} %get-tuple-element.11), channel_id=1, source_target_pairs={{0,13},{1,12},{2,15},{3,14},{4,9},{5,8},{6,11},{7,10},{8,5},{9,4},... | collective-permute-start | bytes 98312 | tf_op jit(solution)/shard_map/ppermute | solution.py:32
  22.6 3.3 %collective-permute-start.8 = (bf16[64,256]{1,0:T(8,128)(2,1)S(1)}, bf16[64,256]{1,0:T(8,128)(2,1)S(1)}, u32[]{:S(2)}, u32[]{:S(2)}) collective-permute-start(bf16[64,256]{1,0:T(8,128)(2,1)S(1)} %get-tuple-element.11), channel_id=1, source_target_pairs={{0,9},{1,8},{2,11},{3,10},{4,13},{5,12},{6,15},{7,14},{8,1},{9,0},... | collective-permute-start | bytes 98312 | tf_op jit(solution)/shard_map/ppermute | solution.py:32
  23.1 3.4 %collective-permute-start.7 = (bf16[64,256]{1,0:T(8,128)(2,1)S(1)}, bf16[64,256]{1,0:T(8,128)(2,1)S(1)}, u32[]{:S(2)}, u32[]{:S(2)}) collective-permute-start(bf16[64,256]{1,0:T(8,128)(2,1)S(1)} %get-tuple-element.11), channel_id=1, source_target_pairs={{0,5},{1,4},{2,7},{3,6},{4,1},{5,0},{6,3},{7,2},{8,13},{9,12},{10,... | collective-permute-start | bytes 98312 | tf_op jit(solution)/shard_map/ppermute | solution.py:32
  25.6 1.2 %collective-permute-start.6 = (bf16[64,256]{1,0:T(8,128)(2,1)S(1)}, bf16[64,256]{1,0:T(8,128)(2,1)S(1)}, u32[]{:S(2)}, u32[]{:S(2)}) collective-permute-start(bf16[64,256]{1,0:T(8,128)(2,1)S(1)} %get-tuple-element.11), channel_id=1, source_target_pairs={{0,1},{1,0},{2,3},{3,2},{4,5},{5,4},{6,7},{7,6},{8,9},{9,8},{10,11... | collective-permute-start | bytes 98312 | tf_op jit(solution)/shard_map/ppermute | solution.py:32
  26.9 3.4 %collective-permute-start.12 = (bf16[64,256]{1,0:T(8,128)(2,1)S(1)}, bf16[64,256]{1,0:T(8,128)(2,1)S(1)}, u32[]{:S(2)}, u32[]{:S(2)}) collective-permute-start(bf16[64,256]{1,0:T(8,128)(2,1)S(1)} %add_add_fusion.1.refs_0_), channel_id=1, source_target_pairs={{0,3},{1,2},{2,1},{3,0},{4,7},{5,6},{6,5},{7,4},{8,11},{9,10},{10,... | collective-permute-start | bytes 98312 | tf_op jit(solution)/shard_map/ppermute | solution.py:25
  27.2 4.1 %collective-permute-start.11 = (bf16[64,256]{1,0:T(8,128)(2,1)S(1)}, bf16[64,256]{1,0:T(8,128)(2,1)S(1)}, u32[]{:S(2)}, u32[]{:S(2)}) collective-permute-start(bf16[64,256]{1,0:T(8,128)(2,1)S(1)} %add_add_fusion.1.refs_0_), channel_id=1, source_target_pairs={{0,2},{1,3},{2,0},{3,1},{4,6},{5,7},{6,4},{7,5},{8,10},{9,11},{10,... | collective-permute-start | bytes 98312 | tf_op jit(solution)/shard_map/ppermute | solution.py:25
  28.7 2.6 %collective-permute-start.10 = (bf16[64,256]{1,0:T(8,128)(2,1)S(1)}, bf16[64,256]{1,0:T(8,128)(2,1)S(1)}, u32[]{:S(2)}, u32[]{:S(2)}) collective-permute-start(bf16[64,256]{1,0:T(8,128)(2,1)S(1)} %add_add_fusion.1.refs_0_), channel_id=1, source_target_pairs={{0,1},{1,0},{2,3},{3,2},{4,5},{5,4},{6,7},{7,6},{8,9},{9,8},{10,11... | collective-permute-start | bytes 98312 | tf_op jit(solution)/shard_map/ppermute | solution.py:25
  28.8 15.9 %copy-start = (bf16[1024,1024]{1,0:T(8,128)(2,1)S(1)}, bf16[1024,1024]{1,0:T(8,128)(2,1)}, u32[]{:S(2)}) copy-start(bf16[1024,1024]{1,0:T(8,128)(2,1)} %refs_5_.3) | copy-start | bytes 6291460
  33.6 4.4 %collective-permute-start.16 = (bf16[16,1152]{1,0:T(8,128)(2,1)S(1)}, bf16[16,1152]{1,0:T(8,128)(2,1)S(1)}, u32[]{:S(2)}, u32[]{:S(2)}) collective-permute-start(bf16[16,1152]{1,0:T(8,128)(2,1)S(1)} %get-tuple-element.12), channel_id=1, source_target_pairs={{0,13},{1,12},{2,15},{3,14},{4,9},{5,8},{6,11},{7,10},{8,5},{9,4},... | collective-permute-start | bytes 110600 | tf_op jit(solution)/shard_map/ppermute | solution.py:32
  34.3 4.0 %collective-permute-start.17 = (bf16[16,1152]{1,0:T(8,128)(2,1)S(1)}, bf16[16,1152]{1,0:T(8,128)(2,1)S(1)}, u32[]{:S(2)}, u32[]{:S(2)}) collective-permute-start(bf16[16,1152]{1,0:T(8,128)(2,1)S(1)} %get-tuple-element.13), channel_id=1, source_target_pairs={{0,9},{1,8},{2,11},{3,10},{4,13},{5,12},{6,15},{7,14},{8,1},{9,0},... | collective-permute-start | bytes 110600 | tf_op jit(solution)/shard_map/ppermute | solution.py:32
  35.9 3.7 %collective-permute-start.18 = (bf16[16,1152]{1,0:T(8,128)(2,1)S(1)}, bf16[16,1152]{1,0:T(8,128)(2,1)S(1)}, u32[]{:S(2)}, u32[]{:S(2)}) collective-permute-start(bf16[16,1152]{1,0:T(8,128)(2,1)S(1)} %get-tuple-element.14), channel_id=1, source_target_pairs={{0,5},{1,4},{2,7},{3,6},{4,1},{5,0},{6,3},{7,2},{8,13},{9,12},{10,... | collective-permute-start | bytes 110600 | tf_op jit(solution)/shard_map/ppermute | solution.py:32
  40.0 3.6 %collective-permute-start.21 = (bf16[16,1152]{1,0:T(8,128)(2,1)S(1)}, bf16[16,1152]{1,0:T(8,128)(2,1)S(1)}, u32[]{:S(2)}, u32[]{:S(2)}) collective-permute-start(bf16[16,1152]{1,0:T(8,128)(2,1)S(1)} %merge.1.refs_0_), channel_id=1, source_target_pairs={{0,3},{1,2},{2,1},{3,0},{4,7},{5,6},{6,5},{7,4},{8,11},{9,10},{10,... | collective-permute-start | bytes 110600 | tf_op jit(solution)/shard_map/ppermute | solution.py:25
  40.7 4.0 %collective-permute-start.20 = (bf16[16,1152]{1,0:T(8,128)(2,1)S(1)}, bf16[16,1152]{1,0:T(8,128)(2,1)S(1)}, u32[]{:S(2)}, u32[]{:S(2)}) collective-permute-start(bf16[16,1152]{1,0:T(8,128)(2,1)S(1)} %merge.1.refs_0_), channel_id=1, source_target_pairs={{0,2},{1,3},{2,0},{3,1},{4,6},{5,7},{6,4},{7,5},{8,10},{9,11},{10,... | collective-permute-start | bytes 110600 | tf_op jit(solution)/shard_map/ppermute | solution.py:25
  41.7 3.0 %collective-permute-start.19 = (bf16[16,1152]{1,0:T(8,128)(2,1)S(1)}, bf16[16,1152]{1,0:T(8,128)(2,1)S(1)}, u32[]{:S(2)}, u32[]{:S(2)}) collective-permute-start(bf16[16,1152]{1,0:T(8,128)(2,1)S(1)} %merge.1.refs_0_), channel_id=1, source_target_pairs={{0,1},{1,0},{2,3},{3,2},{4,5},{5,4},{6,7},{7,6},{8,9},{9,8},{10,11... | collective-permute-start | bytes 110600 | tf_op jit(solution)/shard_map/ppermute | solution.py:25
